TPU v7x, 32 devices: a whole 2x2x4 slice. The times are simulated.
32 devices in a mesh: stream: 32 (over z, y, x, core), item: 1.
Axes of the slice: x: 2, y: 2, z: 4, core: 2. Of those that a mesh axis runs over, the one named last changes fastest.
Arguments:
- event_items: int32 [131072], P('stream'), may hold values from 0 to 262143, as said below
- event_sessions: int32 [131072], P('stream'), may hold values from 0 to 8191, never falling along the last dimension, each value on 1 to 64 neighbouring positions
- sketch_bits: int32 [15, 262144], P(None, 'item'), may hold values from 0 to 262143
Outputs:
- sketch: float32 [128, 256], P('stream')
Inputs may be any that keep to these rules, and one draw needn't show every extreme that they name: `event_items`: item 262144 - 1 occurs at least once.
All inputs are finite; a program needn't handle non-finite values.
Results may differ from a plain program's by a relative error of at most 0.0006.
Values may be sent and summed in bfloat16 or wider, within the bound.
A program may use at most 128 MiB of HBM per device.

v0:
```python
import math

import jax
import jax.numpy as jnp
from jax import lax
from jax.sharding import PartitionSpec as P

SKETCH = 256
WINDOW = 15
ROWS_DEV = 4


def with_halo(shard, sides, width):
    for axis, dim in sides:
        devices, length = (lax.axis_size(axis), shard.shape[dim])
        up = [(i, (i + 1) % devices) for i in range(devices - 1)]
        down = [(j, i) for i, j in up]
        last = lax.slice_in_dim(shard, length - width, length, axis=dim)
        first = lax.slice_in_dim(shard, 0, width, axis=dim)
        before = lax.ppermute(last, axis, up)
        after = lax.ppermute(first, axis, down)
        shard = jnp.concatenate([before, shard, after], axis=dim)
    return shard


def pointwise(count_block, row_margin, col_margin, pair_total):
    log_ratio = (
        jnp.log(jnp.maximum(count_block, 1.0))
        + jnp.log(pair_total)
        - jnp.log(jnp.maximum(row_margin, 1.0))
        - jnp.log(jnp.maximum(col_margin, 1.0))
    )
    return jnp.where(count_block > 0, jnp.maximum(log_ratio, 0.0), 0.0)


def sign_table(bit_block, sketch_width):
    word_count = bit_block.shape[0]
    spread = jnp.repeat(bit_block, 18, axis=0, total_repeat_length=word_count * 18)[:sketch_width]
    bit_shift = (jnp.arange(sketch_width, dtype=jnp.int32) % 18)[:, None]
    return (2 * jnp.bitwise_and(jnp.right_shift(spread, bit_shift), 1) - 1).astype(jnp.float32)


def slab_pairs(ext_items, ext_sessions, row_items):
    extent = ext_items.shape[0]
    own_count = extent - 2 * WINDOW
    own_sessions = ext_sessions[WINDOW : WINDOW + own_count]
    own_items = ext_items[WINDOW : WINDOW + own_count]
    offset = (
        lax.broadcasted_iota(jnp.int32, (own_count, extent), 1)
        - lax.broadcasted_iota(jnp.int32, (own_count, extent), 0)
        - WINDOW
    )
    nearby = (jnp.abs(offset) <= WINDOW) & (offset != 0)
    same_session = own_sessions[:, None] == ext_sessions[None, :]
    banded = (nearby & same_session).astype(jnp.bfloat16)
    row_hot = (
        own_items[None, :] == lax.broadcasted_iota(jnp.int32, (row_items, own_count), 0)
    ).astype(jnp.bfloat16)
    pair_links = lax.dot_general(
        banded, row_hot, (((0,), (1,)), ((), ())), preferred_element_type=jnp.float32
    )
    weights = jnp.sum(banded, axis=0, dtype=jnp.float32)
    return (pair_links, weights)


def tile_block(links_float, ext_items, first_id, col_count):
    local_ids = ext_items - first_id
    in_band = (local_ids >= 0) & (local_ids < col_count)
    return jax.ops.segment_sum(
        jnp.where(in_band[:, None], links_float, 0.0),
        jnp.where(in_band, local_ids, 0),
        num_segments=col_count,
    )


def band_counts(weights, ext_items, first_id, col_count):
    local_ids = ext_items - first_id
    in_band = (local_ids >= 0) & (local_ids < col_count)
    return jax.ops.segment_sum(
        jnp.where(in_band, weights, 0.0), jnp.where(in_band, local_ids, 0), num_segments=col_count
    )


def local(event_items, event_sessions, sketch_bits):
    slab_count = lax.axis_size("stream")
    band_size = sketch_bits.shape[1]
    owned_cols = band_size // slab_count
    row_items = ROWS_DEV * slab_count
    band_start = lax.axis_index("item") * band_size
    own_start = lax.axis_index("stream") * owned_cols
    first_id = band_start + own_start
    total_events = event_items.shape[0] * slab_count
    stacked = jnp.stack([event_items, event_sessions + 1])
    extended = with_halo(stacked, (("stream", 1),), WINDOW)
    initial = (
        jnp.zeros((owned_cols, row_items), jnp.float32),
        jnp.zeros((owned_cols,), jnp.float32),
        jnp.zeros((row_items,), jnp.float32),
        jnp.zeros((), jnp.float32),
    )

    def one_slab(state_inner, slab_events):
        tile_now, col_now, row_now, total_now = state_inner
        pair_links, weights = slab_pairs(slab_events[0], slab_events[1], row_items)
        tile_now = tile_now + tile_block(pair_links, slab_events[0], first_id, owned_cols)
        col_now = col_now + band_counts(weights, slab_events[0], first_id, owned_cols)
        return (
            (
                tile_now,
                col_now,
                row_now + jnp.sum(pair_links, axis=0),
                total_now + jnp.sum(weights),
            ),
            None,
        )

    result, unused = lax.scan(
        one_slab, initial, lax.all_gather(extended[None], "stream", axis=0, tiled=True)
    )
    count_tile, col_margin, row_margin, pair_total = result
    own_bits = lax.dynamic_slice_in_dim(sketch_bits, own_start, owned_cols, 1)
    sign_rows = sign_table(own_bits, SKETCH)
    positive = pointwise(count_tile, row_margin[None, :], col_margin[:, None], pair_total)
    partial_value = lax.dot_general(
        positive,
        sign_rows,
        (((0,), (1,)), ((), ())),
        precision=lax.Precision.HIGHEST,
        preferred_element_type=jnp.float32,
    )
    summed = lax.psum(partial_value, ("stream", "item"))
    own_rows = lax.dynamic_slice_in_dim(summed, lax.axis_index("stream") * ROWS_DEV, ROWS_DEV, 0)
    return own_rows / math.sqrt(total_events)


def solution(mesh):
    placed = (P("stream"), P("stream"), P(None, "item"))
    return jax.shard_map(
        local, mesh=mesh, in_specs=placed, out_specs=P("stream", None), check_vma=False
    )
```

profile of v0, /device:TPU:0, one launch (start us, length us, event | category | flops | bytes accessed | tf_op | source)
XLA Modules:
  0.0 5418.2 jit_solution(12195894624700772319)
XLA Ops:
  76.4 5005.0 %while.20 = (s32[]{:T(128)}, f32[8192,128]{1,0:T(8,128)}, f32[8192]{0:T(1024)S(1)}, f32[128]{0:T(128)S(1)}, f32[]{:T(128)}, /*index=5*/s32[32,2,4126]{2,1,0:T(2,...) while((s32[]{:T(128)}, f32[8192,128]{1,0:T(8,128)}, ...), condition=%wide.region_6.7_spmd.clone, body=%wide.region_0.6_spmd.clone.sunk | while | flops 4666575872 | bytes 9830807 | solution.py:117
  146.4 55.9 %convert_reduce_fusion.3 = (f32[]{:T(128)}, f32[4126]{0:T(1024)S(1)}) fusion(s32[4126]{0:T(1024)S(1)} %dynamic-slice_reduce_fusion.2, s32[4096]{0:T(1024)S(1)} %bitcast.18), kind=kLoop, calls=%fused_computation.3.clone.1 | loop fusion | flops 202797024 | bytes 49396 | tf_op jit(solution)/shard_map/while/body/eval_jaxpr/reduce_sum | solution.py:112
  302.7 55.9 %convert_reduce_fusion.3 = (f32[]{:T(128)}, f32[4126]{0:T(1024)S(1)}) fusion(s32[4126]{0:T(1024)S(1)} %dynamic-slice_reduce_fusion.2, s32[4096]{0:T(1024)S(1)} %bitcast.18), kind=kLoop, calls=%fused_computation.3.clone.1 | loop fusion | flops 202797024 | bytes 49396 | tf_op jit(solution)/shard_map/while/body/eval_jaxpr/reduce_sum | solution.py:112
  459.1 55.9 %convert_reduce_fusion.3 = (f32[]{:T(128)}, f32[4126]{0:T(1024)S(1)}) fusion(s32[4126]{0:T(1024)S(1)} %dynamic-slice_reduce_fusion.2, s32[4096]{0:T(1024)S(1)} %bitcast.18), kind=kLoop, calls=%fused_computation.3.clone.1 | loop fusion | flops 202797024 | bytes 49396 | tf_op jit(solution)/shard_map/while/body/eval_jaxpr/reduce_sum | solution.py:112
  615.5 55.9 %convert_reduce_fusion.3 = (f32[]{:T(128)}, f32[4126]{0:T(1024)S(1)}) fusion(s32[4126]{0:T(1024)S(1)} %dynamic-slice_reduce_fusion.2, s32[4096]{0:T(1024)S(1)} %bitcast.18), kind=kLoop, calls=%fused_computation.3.clone.1 | loop fusion | flops 202797024 | bytes 49396 | tf_op jit(solution)/shard_map/while/body/eval_jaxpr/reduce_sum | solution.py:112
  771.9 55.9 %convert_reduce_fusion.3 = (f32[]{:T(128)}, f32[4126]{0:T(1024)S(1)}) fusion(s32[4126]{0:T(1024)S(1)} %dynamic-slice_reduce_fusion.2, s32[4096]{0:T(1024)S(1)} %bitcast.18), kind=kLoop, calls=%fused_computation.3.clone.1 | loop fusion | flops 202797024 | bytes 49396 | tf_op jit(solution)/shard_map/while/body/eval_jaxpr/reduce_sum | solution.py:112
  928.3 55.9 %convert_reduce_fusion.3 = (f32[]{:T(128)}, f32[4126]{0:T(1024)S(1)}) fusion(s32[4126]{0:T(1024)S(1)} %dynamic-slice_reduce_fusion.2, s32[4096]{0:T(1024)S(1)} %bitcast.18), kind=kLoop, calls=%fused_computation.3.clone.1 | loop fusion | flops 202797024 | bytes 49396 | tf_op jit(solution)/shard_map/while/body/eval_jaxpr/reduce_sum | solution.py:112
  1084.7 55.9 %convert_reduce_fusion.3 = (f32[]{:T(128)}, f32[4126]{0:T(1024)S(1)}) fusion(s32[4126]{0:T(1024)S(1)} %dynamic-slice_reduce_fusion.2, s32[4096]{0:T(1024)S(1)} %bitcast.18), kind=kLoop, calls=%fused_computation.3.clone.1 | loop fusion | flops 202797024 | bytes 49396 | tf_op jit(solution)/shard_map/while/body/eval_jaxpr/reduce_sum | solution.py:112
  1241.2 55.9 %convert_reduce_fusion.3 = (f32[]{:T(128)}, f32[4126]{0:T(1024)S(1)}) fusion(s32[4126]{0:T(1024)S(1)} %dynamic-slice_reduce_fusion.2, s32[4096]{0:T(1024)S(1)} %bitcast.18), kind=kLoop, calls=%fused_computation.3.clone.1 | loop fusion | flops 202797024 | bytes 49396 | tf_op jit(solution)/shard_map/while/body/eval_jaxpr/reduce_sum | solution.py:112
  1397.5 55.9 %convert_reduce_fusion.3 = (f32[]{:T(128)}, f32[4126]{0:T(1024)S(1)}) fusion(s32[4126]{0:T(1024)S(1)} %dynamic-slice_reduce_fusion.2, s32[4096]{0:T(1024)S(1)} %bitcast.18), kind=kLoop, calls=%fused_computation.3.clone.1 | loop fusion | flops 202797024 | bytes 49396 | tf_op jit(solution)/shard_map/while/body/eval_jaxpr/reduce_sum | solution.py:112
  1553.9 55.9 %convert_reduce_fusion.3 = (f32[]{:T(128)}, f32[4126]{0:T(1024)S(1)}) fusion(s32[4126]{0:T(1024)S(1)} %dynamic-slice_reduce_fusion.2, s32[4096]{0:T(1024)S(1)} %bitcast.18), kind=kLoop, calls=%fused_computation.3.clone.1 | loop fusion | flops 202797024 | bytes 49396 | tf_op jit(solution)/shard_map/while/body/eval_jaxpr/reduce_sum | solution.py:112
  1710.3 55.9 %convert_reduce_fusion.3 = (f32[]{:T(128)}, f32[4126]{0:T(1024)S(1)}) fusion(s32[4126]{0:T(1024)S(1)} %dynamic-slice_reduce_fusion.2, s32[4096]{0:T(1024)S(1)} %bitcast.18), kind=kLoop, calls=%fused_computation.3.clone.1 | loop fusion | flops 202797024 | bytes 49396 | tf_op jit(solution)/shard_map/while/body/eval_jaxpr/reduce_sum | solution.py:112
  1866.8 55.9 %convert_reduce_fusion.3 = (f32[]{:T(128)}, f32[4126]{0:T(1024)S(1)}) fusion(s32[4126]{0:T(1024)S(1)} %dynamic-slice_reduce_fusion.2, s32[4096]{0:T(1024)S(1)} %bitcast.18), kind=kLoop, calls=%fused_computation.3.clone.1 | loop fusion | flops 202797024 | bytes 49396 | tf_op jit(solution)/shard_map/while/body/eval_jaxpr/reduce_sum | solution.py:112
  2023.3 55.9 %convert_reduce_fusion.3 = (f32[]{:T(128)}, f32[4126]{0:T(1024)S(1)}) fusion(s32[4126]{0:T(1024)S(1)} %dynamic-slice_reduce_fusion.2, s32[4096]{0:T(1024)S(1)} %bitcast.18), kind=kLoop, calls=%fused_computation.3.clone.1 | loop fusion | flops 202797024 | bytes 49396 | tf_op jit(solution)/shard_map/while/body/eval_jaxpr/reduce_sum | solution.py:112
  2179.7 55.9 %convert_reduce_fusion.3 = (f32[]{:T(128)}, f32[4126]{0:T(1024)S(1)}) fusion(s32[4126]{0:T(1024)S(1)} %dynamic-slice_reduce_fusion.2, s32[4096]{0:T(1024)S(1)} %bitcast.18), kind=kLoop, calls=%fused_computation.3.clone.1 | loop fusion | flops 202797024 | bytes 49396 | tf_op jit(solution)/shard_map/while/body/eval_jaxpr/reduce_sum | solution.py:112
  2336.1 55.9 %convert_reduce_fusion.3 = (f32[]{:T(128)}, f32[4126]{0:T(1024)S(1)}) fusion(s32[4126]{0:T(1024)S(1)} %dynamic-slice_reduce_fusion.2, s32[4096]{0:T(1024)S(1)} %bitcast.18), kind=kLoop, calls=%fused_computation.3.clone.1 | loop fusion | flops 202797024 | bytes 49396 | tf_op jit(solution)/shard_map/while/body/eval_jaxpr/reduce_sum | solution.py:112
  2492.5 55.9 %convert_reduce_fusion.3 = (f32[]{:T(128)}, f32[4126]{0:T(1024)S(1)}) fusion(s32[4126]{0:T(1024)S(1)} %dynamic-slice_reduce_fusion.2, s32[4096]{0:T(1024)S(1)} %bitcast.18), kind=kLoop, calls=%fused_computation.3.clone.1 | loop fusion | flops 202797024 | bytes 49396 | tf_op jit(solution)/shard_map/while/body/eval_jaxpr/reduce_sum | solution.py:112
  2648.9 55.9 %convert_reduce_fusion.3 = (f32[]{:T(128)}, f32[4126]{0:T(1024)S(1)}) fusion(s32[4126]{0:T(1024)S(1)} %dynamic-slice_reduce_fusion.2, s32[4096]{0:T(1024)S(1)} %bitcast.18), kind=kLoop, calls=%fused_computation.3.clone.1 | loop fusion | flops 202797024 | bytes 49396 | tf_op jit(solution)/shard_map/while/body/eval_jaxpr/reduce_sum | solution.py:112
  2805.2 55.9 %convert_reduce_fusion.3 = (f32[]{:T(128)}, f32[4126]{0:T(1024)S(1)}) fusion(s32[4126]{0:T(1024)S(1)} %dynamic-slice_reduce_fusion.2, s32[4096]{0:T(1024)S(1)} %bitcast.18), kind=kLoop, calls=%fused_computation.3.clone.1 | loop fusion | flops 202797024 | bytes 49396 | tf_op jit(solution)/shard_map/while/body/eval_jaxpr/reduce_sum | solution.py:112
  2961.5 55.9 %convert_reduce_fusion.3 = (f32[]{:T(128)}, f32[4126]{0:T(1024)S(1)}) fusion(s32[4126]{0:T(1024)S(1)} %dynamic-slice_reduce_fusion.2, s32[4096]{0:T(1024)S(1)} %bitcast.18), kind=kLoop, calls=%fused_computation.3.clone.1 | loop fusion | flops 202797024 | bytes 49396 | tf_op jit(solution)/shard_map/while/body/eval_jaxpr/reduce_sum | solution.py:112
  3117.9 55.9 %convert_reduce_fusion.3 = (f32[]{:T(128)}, f32[4126]{0:T(1024)S(1)}) fusion(s32[4126]{0:T(1024)S(1)} %dynamic-slice_reduce_fusion.2, s32[4096]{0:T(1024)S(1)} %bitcast.18), kind=kLoop, calls=%fused_computation.3.clone.1 | loop fusion | flops 202797024 | bytes 49396 | tf_op jit(solution)/shard_map/while/body/eval_jaxpr/reduce_sum | solution.py:112
  3274.3 55.9 %convert_reduce_fusion.3 = (f32[]{:T(128)}, f32[4126]{0:T(1024)S(1)}) fusion(s32[4126]{0:T(1024)S(1)} %dynamic-slice_reduce_fusion.2, s32[4096]{0:T(1024)S(1)} %bitcast.18), kind=kLoop, calls=%fused_computation.3.clone.1 | loop fusion | flops 202797024 | bytes 49396 | tf_op jit(solution)/shard_map/while/body/eval_jaxpr/reduce_sum | solution.py:112
  3900.0 55.9 %convert_reduce_fusion.3 = (f32[]{:T(128)}, f32[4126]{0:T(1024)S(1)}) fusion(s32[4126]{0:T(1024)S(1)} %dynamic-slice_reduce_fusion.2, s32[4096]{0:T(1024)S(1)} %bitcast.18), kind=kLoop, calls=%fused_computation.3.clone.1 | loop fusion | flops 202797024 | bytes 49396 | tf_op jit(solution)/shard_map/while/body/eval_jaxpr/reduce_sum | solution.py:112
  5096.0 314.1 %all-reduce.2.cloned.1.call-done = f32[128,256]{1,0:T(8,128)} async-done(((f32[128,256]{1,0:T(8,128)}), f32[128,256]{1,0:T(8,128)}) %all-reduce.2.cloned.1.call-update) | async-done | bytes 131088 | tf_op jit(solution)/shard_map/psum | solution.py:131
  (356 shorter events, 3841.3 us)
Async XLA Ops:
  6.5 67.6 %all-gather.4.cloned.1.call-start = ((), (), s32[]{:S(2)}) async-start(), calls=%async_computation.1 | async-start | bytes 1115136 | tf_op jit(solution)/shard_map/all_gather | solution.py:118
  8.0 4.5 collective-permute-start
  10.4 5.2 collective-permute-start.1
  16.3 5393.8 %all-reduce.2.cloned.1.call-start = ((), (), s32[]{:S(2)}) async-start(), calls=%async_computation | async-start | bytes 262144 | tf_op jit(solution)/shard_map/psum | solution.py:131
  76.4 5005.0 %copy-start = (s32[256]{0:T(256)S(1)}, s32[256]{0:T(256)}, u32[]{:S(2)}) copy-start(s32[256]{0:T(256)} %and_select_fusion.1) | copy-start | bytes 3076
Sparse Core Ops, SparseCore 0:
  16.4 57.6 all-gather.3
  5096.1 313.9 all-reduce.1
where the time goes:
time: 5430 us; the launch traced here: 5420 us
  other arithmetic  3840 us (71%)
  matrix products  1100 us (20%)
  waiting for transfers between devices  366 us (7%)
  local copies, waits for them, and re-layouts  67.9 us (1%)
    reduce_sum x32, other arithmetic, one_slab(): jnp.sum(weights)  1790 us
    dot_general x32, matrix products, slab_pairs(): lax.dot_general(banded, row_hot, (((0,), (1,)), ((), ())), preferred_elem...  1090 us
    scatter-add x32, other arithmetic, tile_block(): jax.ops.segment_sum(jnp.where(in_band[:, None], links_float, 0.0), jnp.wh...  1030 us
    scatter-add x32, other arithmetic, band_counts(): jax.ops.segment_sum(jnp.where(in_band, weights, 0.0), jnp.where(in_band,...  957 us
    psum x1, waiting for transfers between devices, local(): summed = lax.psum(partial_value, ('stream', 'item'))  314 us
  transfers between devices with their start and end apart: 4, of which 3 were waited for; matrix products, arithmetic and copies ran while one was open for 0% of the time, Pallas kernels for 0%

commit v1 on v0

v1 whole, which is shorter than its diff:
```python
import functools
import math

import jax
import jax.numpy as jnp
from jax import lax
from jax.experimental import pallas as pl
from jax.experimental.pallas import tpu as pltpu
from jax.sharding import PartitionSpec as P

WINDOW = 15
ITEM_BITS = 18
LANES = 128
BITS_PER_WORD = 18
BIG = 1.0e6
NT = (((1,), (1,)), ((), ()))
VMEM = pl.BlockSpec(memory_space=pltpu.VMEM)


def one_where(mask):
    return jnp.where(mask, 1.0, 0.0).astype(jnp.bfloat16)


def head_kernel(rows, blocks, code_ref, out_ref):
    ext = rows + 8
    out_ref[...] = jnp.zeros_like(out_ref)
    sub = lax.broadcasted_iota(jnp.int32, (LANES, LANES), 0)
    lane = lax.broadcasted_iota(jnp.int32, (LANES, LANES), 1)
    item_mask = (1 << ITEM_BITS) - 1
    ids = lax.broadcasted_iota(jnp.int32, (ext, LANES), 0)

    def hot(code):
        item = jnp.where(code < 0, rows + 1, code & item_mask)
        item = jnp.where(item >= rows, rows + 1, item)
        return one_where((ids == item) | (ids == rows))

    def step(b, unused):
        own = code_ref[pl.ds(b + 1, 1), :]
        own_session = own >> ITEM_BITS
        links = jnp.zeros((ext, LANES), jnp.float32)
        for o in (-1, 0, 1):
            other = code_ref[pl.ds(b + 1 + o, 1), :]
            other_session = jnp.broadcast_to(other >> ITEM_BITS, (LANES, LANES)).T
            gap = o * LANES + sub - lane
            linked = (other_session == own_session) & (jnp.abs(gap) <= WINDOW) & (gap != 0)
            links += jnp.dot(hot(other), one_where(linked), preferred_element_type=jnp.float32)
        out_ref[...] += lax.dot_general(
            links.astype(jnp.bfloat16), hot(own), NT, preferred_element_type=jnp.float32
        )
        return unused

    lax.fori_loop(0, blocks, step, 0)


def take_windows(code_ref, length, start):
    whole, part = start >> 3, start & 7
    bits = max(1, (length // 8 - 1).bit_length())
    keep = 8 * ((1 << (bits - 1)) + 4)
    value = None
    for bit in reversed(range(bits)):
        step = 8 << bit
        keep = 8 * ((1 << bit) + 4)
        chosen = ((whole >> bit) & 1) == 1
        if value is None:
            low, high = code_ref[0:keep, :], code_ref[step : step + keep, :]
        else:
            low, high = value[0:keep], value[step : step + keep]
        value = jnp.where(chosen, high, low)
    for bit in (2, 1, 0):
        chosen = ((part >> bit) & 1) == 1
        value = jnp.where(chosen, pltpu.roll(value, value.shape[0] - (1 << bit), 0), value)
    return value[0:32]


def tile_kernel(rows, length, half, base_ref, code_ref, count_ref, margin_ref, key_ref):
    item_mask = (1 << ITEM_BITS) - 1
    base = base_ref[0]
    count_ref[...] = jnp.zeros_like(count_ref)
    margin_ref[...] = jnp.zeros_like(margin_ref)
    band = 2 * half
    band_rows = band // LANES
    chunk = 8 * math.gcd(length // 8, 16)

    def fill(c, tops):
        at = pl.multiple_of(c * chunk, chunk)
        item = code_ref[pl.ds(at + 16, chunk), :] & item_mask
        place = (at + lax.broadcasted_iota(jnp.int32, (chunk, LANES), 0)).astype(jnp.float32)
        new = []
        for s in range(2):
            local = item - base - s * band
            mine = (local >= 0) & (local < band) & (item >= rows)
            key_ref[s, pl.ds(at, chunk), :] = jnp.where(mine, place, BIG)
            new.append(tops[s] + jnp.sum(mine.astype(jnp.int32), axis=0, keepdims=True))
        return tuple(new)

    none = jnp.zeros((1, LANES), jnp.int32)
    tally = lax.fori_loop(0, length // chunk, fill, (none, none))
    trips = (jnp.max(jnp.maximum(tally[0], tally[1])) + 1) // 2

    row_ids = lax.broadcasted_iota(jnp.int32, (rows, 2 * LANES), 0).astype(jnp.float32)
    d_ids = lax.broadcasted_iota(jnp.int32, (32, LANES), 0)
    near = (d_ids >= 1) & (d_ids != 16)
    m_ids = lax.broadcasted_iota(jnp.int32, (max(8, band_rows), 2 * LANES), 0)
    l_ids = lax.broadcasted_iota(jnp.int32, (LANES, 2 * LANES), 0)
    tile = min(half, 512)
    t_ids = lax.broadcasted_iota(jnp.int32, (tile, 2 * LANES), 0)

    def body(unused, state):
        out = []
        for s in range(2):
            first, last = state[2 * s], state[2 * s + 1]
            key = key_ref[s]
            next_first = jnp.min(jnp.where(key > first, key, BIG), axis=0, keepdims=True)
            next_last = jnp.max(jnp.where(key < last, key, -1.0), axis=0, keepdims=True)
            first_ok = next_first < last
            last_ok = next_last > next_first
            out += [next_first, next_last]
            heads, weights, locals_ = [], [], []
            for at, ok in ((next_first, first_ok), (next_last, last_ok)):
                start = jnp.where(ok, at, 0.0).astype(jnp.int32)
                window = take_windows(code_ref, length, start)
                item, session = window & item_mask, window >> ITEM_BITS
                linked = (session == session[16:17]) & near & ok
                heads.append(jnp.where(linked & (item < rows), item, -1).astype(jnp.float32))
                weights.append(jnp.sum(jnp.where(linked, 1.0, 0.0), axis=0, keepdims=True))
                locals_.append(item[16:17] - base - s * band)
            head = jnp.concatenate(heads, axis=1)
            weight = jnp.concatenate(weights, axis=1)
            local = jnp.concatenate(locals_, axis=1)
            links = jnp.zeros((rows, 2 * LANES), jnp.float32)
            for d in range(1, 32):
                if d != 16:
                    links += jnp.where(row_ids == head[d : d + 1], 1.0, 0.0)
            upper = local >= half
            pair = jnp.concatenate(
                [jnp.where(upper, 0.0, links), jnp.where(upper, links, 0.0)], axis=0
            ).astype(jnp.bfloat16)
            inner = jnp.where(upper, local - half, local)
            for t in range(half // tile):
                hot = one_where(t_ids + t * tile == inner)
                count_ref[s, :, t * tile : (t + 1) * tile] += lax.dot_general(
                    pair, hot, NT, preferred_element_type=jnp.float32
                )
            coarse = jnp.where(m_ids == (local >> 7), weight, 0.0).astype(jnp.bfloat16)
            fine = one_where(l_ids == (local & (LANES - 1)))
            margin_ref[s] += lax.dot_general(coarse, fine, NT, preferred_element_type=jnp.float32)
        return tuple(out)

    low = jnp.full((1, LANES), -1.0, jnp.float32)
    high = jnp.full((1, LANES), BIG, jnp.float32)
    lax.fori_loop(0, trips, body, (low, high, low, high))


def sketch_kernel(rows, half, width, scale, flag_ref, count_ref, margin_ref, head_ref, bits_ref, out_ref, log_ref):
    flag = flag_ref[0]
    band_rows = 2 * half // LANES
    row_margin = head_ref[rows : rows + 1, 0:rows]
    first_row = lax.broadcasted_iota(jnp.int32, margin_ref.shape[1:], 0) == 0
    log_ref[0] = jnp.log(jnp.maximum(margin_ref[0] + jnp.where(first_row, row_margin * flag, 0.0), 1.0))
    log_ref[1] = jnp.log(jnp.maximum(margin_ref[1], 1.0))
    row_term = jnp.log(head_ref[rows : rows + 1, rows : rows + 1]) - jnp.log(
        jnp.maximum(head_ref[0:rows, rows : rows + 1], 1.0)
    )
    tile = min(half, 512)
    out_ref[...] = jnp.zeros_like(out_ref)
    shift = lax.broadcasted_iota(jnp.int32, (8, tile), 0)
    head_block = head_ref[0:rows, 0:rows] * flag
    groups = []
    for g in range(width // 8):
        word = 8 * g // BITS_PER_WORD
        split = (word + 1) * BITS_PER_WORD - 8 * g
        groups.append((word, split, 8 * g - word * BITS_PER_WORD))

    def block(s, h, t):
        at = pl.multiple_of(t * tile, tile)
        counts = count_ref[s, h * rows : (h + 1) * rows, pl.ds(at, tile)]
        if s == 0 and h == 0:
            on = jnp.where(t == 0, 1.0, 0.0)
            extra = head_block * on
            if tile > rows:
                extra = jnp.concatenate([extra, jnp.zeros((rows, tile - rows), jnp.float32)], axis=1)
            counts = counts + extra
        first_log = h * (half // LANES) + t * (tile // LANES)
        col_log = jnp.concatenate(
            [log_ref[s, pl.ds(first_log + n, 1), :] for n in range(tile // LANES)], axis=1
        )
        ratio = jnp.log(jnp.maximum(counts, 1.0)) + row_term - col_log
        positive = jnp.where(counts > 0, jnp.maximum(ratio, 0.0), 0.0)
        upper = positive.astype(jnp.bfloat16)
        lower = (positive - upper.astype(jnp.float32)).astype(jnp.bfloat16)
        bit_at = pl.multiple_of(s * 2 * half + h * half + t * tile, tile)
        words = bits_ref[:, pl.ds(bit_at, tile)]
        parts = []
        for word, split, offset in groups:
            now = jnp.broadcast_to(words[word : word + 1], (8, tile))
            where_bit = shift + offset
            if split < 8:
                after = jnp.broadcast_to(words[word + 1 : word + 2], (8, tile))
                now = jnp.where(shift >= split, after, now)
                where_bit = jnp.where(shift >= split, shift - split, where_bit)
            parts.append(jnp.where(((now >> where_bit) & 1) == 1, 1.0, -1.0))
        signs = jnp.concatenate(parts, axis=0).astype(jnp.bfloat16)
        both = jnp.concatenate([upper, lower], axis=0)
        product = lax.dot_general(both, signs, NT, preferred_element_type=jnp.float32)
        out_ref[...] += product[0:rows] + product[rows:]

    for s in range(2):
        for h in range(2):

            def step(t, unused, s=s, h=h):
                block(s, h, t)
                return unused

            lax.fori_loop(0, half // tile, step, 0)
    out_ref[...] = out_ref[...] * scale


def local(event_items, event_sessions, sketch_bits):
    slabs = lax.axis_size("stream")
    slab = event_items.shape[0]
    total_events = slab * slabs
    words, band_size = sketch_bits.shape
    owned = band_size // slabs
    rows, width, half = 128, 256, owned // 4
    me = lax.axis_index("stream")
    own_start = me * owned
    first_id = lax.axis_index("item") * band_size + own_start
    blocks = slab // LANES
    length = total_events // LANES

    events = lax.all_gather(jnp.stack([event_items, event_sessions])[None], "stream", axis=0, tiled=True)
    code = events[:, 0] | (events[:, 1] << ITEM_BITS)
    flat = code.reshape(length, LANES)
    padded = jnp.pad(flat, ((1, 1), (0, 0)), constant_values=-1)
    own = lax.dynamic_slice_in_dim(padded, me * blocks, blocks + 2, 0)
    head = pl.pallas_call(
        functools.partial(head_kernel, rows, blocks),
        out_shape=jax.ShapeDtypeStruct((rows + 8, rows + 8), jnp.float32),
        in_specs=[VMEM],
        out_specs=VMEM,
        name="head_counts",
    )(own)
    head = lax.psum(head, "stream")

    deep = code.reshape(LANES, length).T
    before = jnp.pad(deep[length - 16 :, :-1], ((0, 0), (1, 0)), constant_values=-1)
    after = jnp.pad(deep[:16, 1:], ((0, 0), (0, 1)), constant_values=-1)
    deep = jnp.concatenate([before, deep, after], axis=0)
    band_rows = max(8, 2 * half // LANES)
    counts, margins = pl.pallas_call(
        functools.partial(tile_kernel, rows, length, half),
        out_shape=(
            jax.ShapeDtypeStruct((2, 2 * rows, half), jnp.float32),
            jax.ShapeDtypeStruct((2, band_rows, LANES), jnp.float32),
        ),
        in_specs=[pl.BlockSpec(memory_space=pltpu.SMEM), VMEM],
        out_specs=(VMEM, VMEM),
        scratch_shapes=[pltpu.VMEM((2, length, LANES), jnp.float32)],
        cost_estimate=pl.CostEstimate(flops=40_000_000_000, bytes_accessed=5_000_000, transcendentals=0),
        name="tile_counts",
    )(first_id.astype(jnp.int32)[None], deep)

    own_bits = lax.dynamic_slice_in_dim(sketch_bits, own_start, owned, 1)
    own_bits = jnp.pad(own_bits, ((0, 16 - words), (0, 0)))
    flag = jnp.where(first_id == 0, 1.0, 0.0).astype(jnp.float32)[None]
    partial_sketch = pl.pallas_call(
        functools.partial(sketch_kernel, rows, half, width, 1.0 / math.sqrt(total_events)),
        out_shape=jax.ShapeDtypeStruct((rows, width), jnp.float32),
        in_specs=[pl.BlockSpec(memory_space=pltpu.SMEM)] + [VMEM] * 4,
        out_specs=VMEM,
        scratch_shapes=[pltpu.VMEM((2, band_rows, LANES), jnp.float32)],
        name="sketch_tile",
    )(flag, counts, margins, head, own_bits)
    own_rows = lax.psum_scatter(partial_sketch, "stream", scatter_dimension=0, tiled=True)
    if lax.axis_size("item") > 1:
        own_rows = lax.psum(own_rows, "item")
    return own_rows


def solution(mesh):
    placed = (P("stream"), P("stream"), P(None, "item"))
    return jax.shard_map(
        local, mesh=mesh, in_specs=placed, out_specs=P("stream", None), check_vma=False
    )
```

time: 5430 us -> 351 us (0.06)
  other arithmetic: 3840 us -> 5.85 us
  matrix products: 1100 us -> 0 us
  waiting for transfers between devices: 366 us -> 280 us
  local copies, waits for them, and re-layouts: 67.9 us -> 4.25 us
    scatter-add x64 -> x0, other arithmetic: 1990 us -> none  [the longest x32 1030 us: tile_block(): jax.ops.segment_sum(jnp.where(in_band[:, None], links_float, 0.0), jnp.wh...]
    reduce_sum x64 -> x0, other arithmetic: 1800 us -> none  [the longest x32 1790 us: one_slab(): jnp.sum(weights)]
    dot_general x33 -> x0, matrix products: 1100 us -> none  [the longest x32 1090 us: slab_pairs(): lax.dot_general(banded, row_hot, (((0,), (1,)), ((), ())), preferred_elem...]
    psum x1, waiting for transfers between devices: 314 us -> 95.9 us  [local(): head = lax.psum(head, 'stream')]
    unnamed x2 -> x4, waiting for transfers between devices: 0.03 us -> 127 us
    slice x64 -> x1, local copies, waits for them, and re-layouts: 57.4 us -> 0.07 us  [local(): deep[length - 16:, :-1]]
  transfers between devices with their start and end apart: 4 -> 3, of which waited for: 3 -> 3; matrix products, arithmetic and copies ran while one was open for 0% -> 1% of each run, Pallas kernels for 0% -> 7%
where the time goes in v1:
time: 351 us
  waiting for transfers between devices  280 us (80%)
  Pallas kernels  47.7 us (14%)
  between operations  13.1 us (4%)
  other arithmetic  5.85 us (2%)
  local copies, waits for them, and re-layouts  4.25 us (1%)
    unnamed x4, waiting for transfers between devices  127 us
    psum x1, waiting for transfers between devices, local(): head = lax.psum(head, 'stream')  95.9 us
    all_gather x1, waiting for transfers between devices, local(): lax.all_gather(jnp.stack([event_items, event_sessions])[None], 'stream',...  56.6 us
    pallas_call x1, Pallas kernels, local(): pl.pallas_call(functools.partial(tile_kernel, rows, length, half), out_sh...  24 us
    pallas_call x1, Pallas kernels, local(): pl.pallas_call(functools.partial(head_kernel, rows, blocks), out_shape=ja...  15.1 us
    pallas_call x1, Pallas kernels, local(): pl.pallas_call(functools.partial(sketch_kernel, rows, half, width, 1.0 /...  8.61 us
  transfers between devices with their start and end apart: 3, of which 3 were waited for; matrix products, arithmetic and copies ran while one was open for 1% of the time, Pallas kernels for 7%

profile of v1, /device:TPU:0, one launch (start us, length us, event | category | flops | bytes accessed | tf_op | source)
XLA Modules:
  0.0 351.0 jit_solution(7800019716353118003)
XLA Ops:
  6.5 0.0 all-gather.4.cloned.1.call-start
  6.5 1.4 add_bitcast_fusion
  7.9 0.0 all-gather.4.cloned.1.call-update
  7.9 0.0 all-reduce.8.cloned.1.call-start
  8.0 1.1 constant_dynamic-slice_fusion.1
  9.1 0.8 pad.19.bits_ref
  9.9 56.6 %all-gather.4.cloned.1.call-done = s32[32,2,4096]{2,1,0:T(2,128)} async-done(((s32[1,2,4096]{2,1,0:T(2,128)}), s32[32,2,4096]{2,1,0:T(2,128)}) %all-gather.4.cloned.1.call-update) | async-done | bytes 1048592 | tf_op jit(solution)/shard_map/all_gather | solution.py:231
  66.6 3.6 %fusion.1 = (s32[32,4096]{1,0:T(8,128)S(1)}, s32[32,1,4096]{2,1,0:T(1,128)S(1)}) fusion(s32[32,2,4096]{2,1,0:T(2,128)} %all-gather.4.cloned.1.call-done), kind=kLoop, calls=%fused_computation.10 | loop fusion | flops 262144 | bytes 2097152 | tf_op jit(solution)/shard_map/or | solution.py:232
  70.1 0.1 or.12
  70.3 0.2 copy.5
  70.5 0.1 fusion.3
  70.6 0.6 pad_dynamic-slice_fusion.code_ref
  71.2 15.1 %head_counts.1 = f32[136,136]{1,0:T(8,128)} custom-call(s32[34,128]{1,0:T(8,128)} %pad_dynamic-slice_fusion.code_ref), custom_call_target="tpu_custom_call" | custom-call | tf_op jit(solution)/shard_map/head_counts/pallas_call | solution.py:236
  86.3 0.0 all-reduce.8.cloned.1.call-update
  86.4 0.0 all-reduce.10.cloned.1.call-start
  86.4 0.9 select_add_fusion.code_ref
  87.3 24.0 %tile_counts.1 = (f32[2,256,2048]{2,1,0:T(8,128)}, f32[2,32,128]{2,1,0:T(8,128)}) custom-call(s32[1]{0:T(128)} %bitcast.1.base_ref, s32[1056,128]{1,0:T(8,128)} %select_add_fusion.code_ref), custom_call_target="tpu_custom_call" | custom-call | flops 40000000000 | bytes 5000000 | tf_op jit(solution)/shard_map/tile_counts/pallas_call | solution.py:250
  111.3 95.9 %all-reduce.8.cloned.1.call-done.head_ref = f32[136,136]{1,0:T(8,128)} async-done(((f32[136,136]{1,0:T(8,128)}), f32[136,136]{1,0:T(8,128)}) %all-reduce.8.cloned.1.call-update) | async-done | bytes 74000 | tf_op jit(solution)/shard_map/psum | solution.py:243
  207.2 8.6 %sketch_tile.1 = f32[128,256]{1,0:T(8,128)} custom-call(f32[1]{0:T(128)} %bitcast.flag_ref, f32[2,256,2048]{2,1,0:T(8,128)} %get-tuple-element.7.count_ref, f32[2,32,128]{2,1,0:T(8,128)} %get-tuple-element.8.margin_ref, f32[136,136]{1,0:T(8,128)} %all-reduce.8.cloned.1.call-done.head_ref, s32[16,8192]{1,0:T(8,128)} %pad.19.bits_ref), custom_call_target="tpu_custom_call" | custom-call | tf_op jit(solution)/shard_map/sketch_tile/pallas_call | solution.py:266
  215.8 0.0 all-reduce.10.cloned.1.call-update
  215.9 127.3 %all-reduce.10.cloned.1.call-done = f32[128,256]{1,0:T(8,128)} async-done(((f32[128,256]{1,0:T(8,128)}), f32[128,256]{1,0:T(8,128)}) %all-reduce.10.cloned.1.call-update) | async-done | bytes 131088
  343.1 1.3 constant_dynamic-slice_fusion
Async XLA Ops:
  6.5 60.0 %all-gather.4.cloned.1.call-start = ((), (), s32[]{:S(2)}) async-start(), calls=%async_computation.1 | async-start | bytes 1081344 | tf_op jit(solution)/shard_map/all_gather | solution.py:231
  7.9 199.3 %all-reduce.8.cloned.1.call-start = ((), (), s32[]{:S(2)}) async-start(), calls=%async_computation | async-start | bytes 278528 | tf_op jit(solution)/shard_map/psum | solution.py:243
  86.4 256.8 %all-reduce.10.cloned.1.call-start = ((), (), s32[]{:S(2)}) async-start(), calls=%async_computation.2 | async-start | bytes 262144
Sparse Core Ops, SparseCore 0:
  10.2 56.3 all-gather.3
  86.5 120.6 all-reduce.7
  216.0 127.1 all-reduce.9

commit v2 on v1

v2 whole, which is shorter than its diff:
```python
import functools
import math

import jax
import jax.numpy as jnp
from jax import lax
from jax.experimental import pallas as pl
from jax.experimental.pallas import tpu as pltpu
from jax.sharding import PartitionSpec as P

WINDOW = 15
ITEM_BITS = 18
LANES = 128
BITS_PER_WORD = 18
BIG = 1.0e6
NT = (((1,), (1,)), ((), ()))
VMEM = pl.BlockSpec(memory_space=pltpu.VMEM)


def one_where(mask):
    return jnp.where(mask, 1.0, 0.0).astype(jnp.bfloat16)


def greet_all(slabs, me):
    barrier = pltpu.get_barrier_semaphore()

    def signal(k, unused):
        pl.semaphore_signal(
            barrier, inc=1, device_id={"stream": lax.rem(me + k, slabs)}, device_id_type=pl.DeviceIdType.MESH
        )
        return unused

    lax.fori_loop(1, slabs, signal, 0)
    return barrier


def send(src, dst, send_sem, recv_sem, to):
    return pltpu.make_async_remote_copy(
        src_ref=src,
        dst_ref=dst,
        send_sem=send_sem,
        recv_sem=recv_sem,
        device_id={"stream": to},
        device_id_type=pl.DeviceIdType.MESH,
    )


def each(low, high, do):
    def step(k, unused):
        do(k)
        return unused

    lax.fori_loop(low, high, step, 0)


def exchange(slabs, me, out_ref, in_ref, send_sems, recv_sems, start):
    def copy(k):
        to = lax.rem(me + k, slabs)
        return send(out_ref.at[to], in_ref.at[me], send_sems.at[k], recv_sems.at[k], to)

    if start:
        each(1, slabs, lambda k: copy(k).start())
        in_ref[me] = out_ref[me]
    else:
        each(1, slabs, lambda k: copy(k).wait())


def gather_kernel(
    slabs, rows, blocks, own_ref, all_ref, head_ref, halo_ref, item_ref, session_ref, links_ref, total_ref,
    head_out, head_in, far_send, far_recv, near_send, near_recv, halo_send, halo_recv, head_send, head_recv,
):
    me = lax.axis_index("stream")
    partner = me + 1 - 2 * lax.rem(me, 2)
    after, before = lax.rem(me + 1, slabs), lax.rem(me + slabs - 1, slabs)
    barrier = greet_all(slabs, me)
    pl.semaphore_wait(barrier, slabs - 1)

    low_halo = send(own_ref.at[:, blocks - 8 : blocks], halo_ref.at[0], halo_send.at[0], halo_recv.at[0], after)
    high_halo = send(own_ref.at[:, 0:8], halo_ref.at[1], halo_send.at[1], halo_recv.at[1], before)
    low_halo.start()
    high_halo.start()

    def far(k):
        return send(own_ref, all_ref.at[me], far_send.at[k], far_recv.at[k], lax.rem(me + 2 * k, slabs))

    def near(k):
        source = lax.rem(me + 2 * slabs - 2 * k, slabs)
        return send(all_ref.at[source], all_ref.at[source], near_send.at[k], near_recv.at[k], partner)

    own_near = send(own_ref, all_ref.at[me], near_send.at[0], near_recv.at[0], partner)
    own_near.start()
    each(1, slabs // 2, lambda k: far(k).start())
    all_ref[me] = own_ref[...]

    item_ref[8 : 8 + blocks] = own_ref[0]
    session_ref[8 : 8 + blocks] = own_ref[1]
    low_halo.wait()
    high_halo.wait()
    item_ref[0:8] = halo_ref[0, 0]
    item_ref[8 + blocks : 16 + blocks] = halo_ref[1, 0]
    session_ref[0:8] = jnp.where(me == 0, -1, halo_ref[0, 1])
    session_ref[8 + blocks : 16 + blocks] = jnp.where(me == slabs - 1, -1, halo_ref[1, 1])

    sub = lax.broadcasted_iota(jnp.int32, (LANES, LANES), 0)
    lane = lax.broadcasted_iota(jnp.int32, (LANES, LANES), 1)
    low_lane = lax.broadcasted_iota(jnp.int32, (1, LANES), 1) < LANES // 2
    ids = lax.broadcasted_iota(jnp.int32, (rows, LANES), 0)
    gaps = (sub - LANES // 2 - lane, sub + LANES // 2 - lane)
    in_reach = [(jnp.abs(gap) <= WINDOW) & (gap != 0) for gap in gaps]
    ones = jnp.ones((8, 2 * LANES), jnp.float32).astype(jnp.bfloat16)
    links_ref[...] = jnp.zeros_like(links_ref)
    total_ref[...] = jnp.zeros_like(total_ref)

    def block(b, unused):
        def around(ref):
            turned = [pltpu.roll(ref[pl.ds(b + o, 1)], LANES // 2, 1) for o in (7, 8, 9)]
            return (
                jnp.where(low_lane, turned[0], turned[1]),
                jnp.where(low_lane, turned[1], turned[2]),
            )

        own_item, own_session = item_ref[pl.ds(b + 8, 1)], session_ref[pl.ds(b + 8, 1)]
        hot = jnp.concatenate([one_where(ids == item) for item in around(item_ref)], axis=1)
        linked = jnp.concatenate(
            [
                one_where((jnp.broadcast_to(session, (LANES, LANES)).T == own_session) & reach)
                for session, reach in zip(around(session_ref), in_reach)
            ],
            axis=0,
        )
        links = jnp.dot(jnp.concatenate([hot, ones], axis=0), linked, preferred_element_type=jnp.float32)
        links_ref[...] += lax.dot_general(
            links.astype(jnp.bfloat16), one_where(ids == own_item), NT, preferred_element_type=jnp.float32
        )
        total_ref[...] += links[rows:]
        return unused

    lax.fori_loop(0, blocks, block, 0, unroll=4)

    share = rows // slabs
    tail = jnp.concatenate([links_ref[rows : rows + 1], total_ref[0:1]], axis=0)
    for d in range(slabs):
        head_out[d, 0:share] = links_ref[d * share : (d + 1) * share]
        head_out[d, share : share + 2] = tail
        head_out[d, share + 2 : 8] = jnp.zeros((6 - share, LANES), jnp.float32)

    exchange(slabs, me, head_out, head_in, head_send, head_recv, True)

    def forward(k):
        far(k).wait_recv()
        near(k).start()

    each(1, slabs // 2, forward)
    exchange(slabs, me, head_out, head_in, head_send, head_recv, False)
    head_ref[...] = jnp.sum(head_in[...], axis=0)
    own_near.wait()
    each(1, slabs // 2, lambda k: near(k).wait())
    each(1, slabs // 2, lambda k: far(k).wait_send())


def take_windows(code_ref, length, start):
    whole, part = start >> 3, start & 7
    bits = max(1, (length // 8 - 1).bit_length())
    keep = 8 * ((1 << (bits - 1)) + 4)
    value = None
    for bit in reversed(range(bits)):
        step = 8 << bit
        keep = 8 * ((1 << bit) + 4)
        chosen = ((whole >> bit) & 1) == 1
        if value is None:
            low, high = code_ref[0:keep, :], code_ref[step : step + keep, :]
        else:
            low, high = value[0:keep], value[step : step + keep]
        value = jnp.where(chosen, high, low)
    for bit in (2, 1, 0):
        chosen = ((part >> bit) & 1) == 1
        value = jnp.where(chosen, pltpu.roll(value, value.shape[0] - (1 << bit), 0), value)
    return value[0:32]


def tile_kernel(rows, length, half, base_ref, all_ref, count_ref, margin_ref, flat_ref, code_ref, key_ref):
    item_mask = (1 << ITEM_BITS) - 1
    base = base_ref[0]
    count_ref[...] = jnp.zeros_like(count_ref)
    margin_ref[...] = jnp.zeros_like(margin_ref)
    band = 2 * half
    band_rows = band // LANES
    chunk = 8 * math.gcd(length // 8, 16)
    blocks = all_ref.shape[2]
    for n in range(all_ref.shape[0]):
        flat_ref[n * blocks : (n + 1) * blocks] = all_ref[n, 0] | (all_ref[n, 1] << ITEM_BITS)
    per = length // LANES
    for r in range(per):
        code_ref[16 + r * LANES : 16 + (r + 1) * LANES] = flat_ref[pl.ds(r, LANES, stride=per), :].T
    lane = lax.broadcasted_iota(jnp.int32, (16, LANES), 1)
    code_ref[0:16] = jnp.where(lane == 0, -1, pltpu.roll(code_ref[length : length + 16], 1, 1))
    code_ref[length + 16 : length + 32] = jnp.where(
        lane == LANES - 1, -1, pltpu.roll(code_ref[16:32], LANES - 1, 1)
    )

    def fill(c, tops):
        at = pl.multiple_of(c * chunk, chunk)
        item = code_ref[pl.ds(at + 16, chunk), :] & item_mask
        place = (at + lax.broadcasted_iota(jnp.int32, (chunk, LANES), 0)).astype(jnp.float32)
        new = []
        for s in range(2):
            local = item - base - s * band
            mine = (local >= 0) & (local < band) & (item >= rows)
            key_ref[s, pl.ds(at, chunk), :] = jnp.where(mine, place, BIG)
            new.append(tops[s] + jnp.sum(mine.astype(jnp.int32), axis=0, keepdims=True))
        return tuple(new)

    none = jnp.zeros((1, LANES), jnp.int32)
    tally = lax.fori_loop(0, length // chunk, fill, (none, none))
    trips = (jnp.max(jnp.maximum(tally[0], tally[1])) + 1) // 2

    row_ids = lax.broadcasted_iota(jnp.int32, (rows, 2 * LANES), 0).astype(jnp.float32)
    d_ids = lax.broadcasted_iota(jnp.int32, (32, LANES), 0)
    near = (d_ids >= 1) & (d_ids != 16)
    m_ids = lax.broadcasted_iota(jnp.int32, (max(8, band_rows), 2 * LANES), 0)
    l_ids = lax.broadcasted_iota(jnp.int32, (LANES, 2 * LANES), 0)
    tile = min(half, 512)
    t_ids = lax.broadcasted_iota(jnp.int32, (tile, 2 * LANES), 0)

    def body(unused, state):
        out = []
        for s in range(2):
            first, last = state[2 * s], state[2 * s + 1]
            key = key_ref[s]
            next_first = jnp.min(jnp.where(key > first, key, BIG), axis=0, keepdims=True)
            next_last = jnp.max(jnp.where(key < last, key, -1.0), axis=0, keepdims=True)
            first_ok = next_first < last
            last_ok = next_last > next_first
            out += [next_first, next_last]
            heads, weights, locals_ = [], [], []
            for at, ok in ((next_first, first_ok), (next_last, last_ok)):
                start = jnp.where(ok, at, 0.0).astype(jnp.int32)
                window = take_windows(code_ref, length, start)
                item, session = window & item_mask, window >> ITEM_BITS
                linked = (session == session[16:17]) & near & ok
                heads.append(jnp.where(linked & (item < rows), item, -1).astype(jnp.float32))
                weights.append(jnp.sum(jnp.where(linked, 1.0, 0.0), axis=0, keepdims=True))
                locals_.append(item[16:17] - base - s * band)
            head = jnp.concatenate(heads, axis=1)
            weight = jnp.concatenate(weights, axis=1)
            local = jnp.concatenate(locals_, axis=1)
            links = jnp.zeros((rows, 2 * LANES), jnp.float32)
            for d in range(1, 32):
                if d != 16:
                    links += jnp.where(row_ids == head[d : d + 1], 1.0, 0.0)
            upper = local >= half
            pair = jnp.concatenate(
                [jnp.where(upper, 0.0, links), jnp.where(upper, links, 0.0)], axis=0
            ).astype(jnp.bfloat16)
            inner = jnp.where(upper, local - half, local)
            for t in range(half // tile):
                hot = one_where(t_ids + t * tile == inner)
                count_ref[s, :, t * tile : (t + 1) * tile] += lax.dot_general(
                    pair, hot, NT, preferred_element_type=jnp.float32
                )
            coarse = jnp.where(m_ids == (local >> 7), weight, 0.0).astype(jnp.bfloat16)
            fine = one_where(l_ids == (local & (LANES - 1)))
            margin_ref[s] += lax.dot_general(coarse, fine, NT, preferred_element_type=jnp.float32)
        return tuple(out)

    low = jnp.full((1, LANES), -1.0, jnp.float32)
    high = jnp.full((1, LANES), BIG, jnp.float32)
    lax.fori_loop(0, trips, body, (low, high, low, high))


def sketch_kernel(
    slabs, rows, half, width, scale, count_ref, margin_ref, head_ref, bits_ref, out_ref,
    log_ref, own_bits, head_bits, acc_ref, send_ref, recv_ref, bit_sems, send_sems, recv_sems,
):
    me = lax.axis_index("stream")
    barrier = greet_all(slabs, me)
    owned = 4 * half
    share = rows // slabs
    tile = min(half, 512)
    bit_copy = pltpu.make_async_copy(
        bits_ref.at[:, pl.ds(pl.multiple_of(me * owned, owned), owned)], own_bits, bit_sems.at[0]
    )
    head_copy = pltpu.make_async_copy(bits_ref.at[:, 0:rows], head_bits, bit_sems.at[1])
    bit_copy.start()
    head_copy.start()

    log_ref[...] = jnp.log(jnp.maximum(margin_ref[...], 1.0))
    row_log = jnp.log(jnp.maximum(head_ref[share : share + 1], 1.0))
    column_log = jnp.broadcast_to(row_log, (rows, LANES)).T
    total_log = jnp.log(jnp.sum(head_ref[share + 1 : share + 2], axis=1, keepdims=True))
    row_term = total_log - column_log[:, 0:1]
    groups = []
    for g in range(width // 8):
        word = 8 * g // BITS_PER_WORD
        groups.append((word, (word + 1) * BITS_PER_WORD - 8 * g, 8 * g - word * BITS_PER_WORD))

    def product(positive, words):
        size = words.shape[1]
        shift = lax.broadcasted_iota(jnp.int32, (8, size), 0)
        upper = positive.astype(jnp.bfloat16)
        lower = (positive - upper.astype(jnp.float32)).astype(jnp.bfloat16)
        parts = []
        for word, split, offset in groups:
            now = jnp.broadcast_to(words[word : word + 1], (8, size))
            where_bit = shift + offset
            if split < 8:
                later = jnp.broadcast_to(words[word + 1 : word + 2], (8, size))
                now = jnp.where(shift >= split, later, now)
                where_bit = jnp.where(shift >= split, shift - split, where_bit)
            parts.append(jnp.where(((now >> where_bit) & 1) == 1, 1.0, -1.0))
        signs = jnp.concatenate(parts, axis=0).astype(jnp.bfloat16)
        both = jnp.concatenate([upper, lower], axis=0)
        value = lax.dot_general(both, signs, NT, preferred_element_type=jnp.float32)
        return value[0:rows] + value[rows:]

    head_copy.wait()
    row = lax.broadcasted_iota(jnp.int32, (8, LANES), 0)
    shared = jnp.concatenate(
        [jnp.where(row < share, head_ref[...], 0.0), jnp.zeros((rows - 8, LANES), jnp.float32)], axis=0
    )
    shared = pltpu.roll(shared, me * share, 0)
    ratio = jnp.log(jnp.maximum(shared, 1.0)) + total_log - row_log - column_log
    first_band = jnp.where(lax.axis_index("item") == 0, 1.0, 0.0)
    positive = jnp.where(shared > 0, jnp.maximum(ratio, 0.0), 0.0) * first_band
    acc_ref[...] = product(positive.T, head_bits[...])
    bit_copy.wait()

    for s in range(2):
        for h in range(2):

            def step(t, unused, s=s, h=h):
                at = pl.multiple_of(t * tile, tile)
                counts = count_ref[s, h * rows : (h + 1) * rows, pl.ds(at, tile)]
                first_log = h * (half // LANES) + t * (tile // LANES)
                col_log = jnp.concatenate(
                    [log_ref[s, pl.ds(first_log + n, 1), :] for n in range(tile // LANES)], axis=1
                )
                ratio = jnp.log(jnp.maximum(counts, 1.0)) + row_term - col_log
                positive = jnp.where(counts > 0, jnp.maximum(ratio, 0.0), 0.0)
                bit_at = pl.multiple_of(s * 2 * half + h * half + t * tile, tile)
                acc_ref[...] += product(positive, own_bits[:, pl.ds(bit_at, tile)])
                return unused

            lax.fori_loop(0, half // tile, step, 0)

    cuts = width // LANES
    for d in range(slabs):
        for c in range(cuts):
            send_ref[d, c * share : (c + 1) * share] = (
                acc_ref[d * share : (d + 1) * share, c * LANES : (c + 1) * LANES] * scale
            )
    pl.semaphore_wait(barrier, slabs - 1)
    exchange(slabs, me, send_ref, recv_ref, send_sems, recv_sems, True)
    exchange(slabs, me, send_ref, recv_ref, send_sems, recv_sems, False)
    summed = jnp.sum(recv_ref[...], axis=0)
    out_ref[...] = jnp.concatenate([summed[c * share : (c + 1) * share] for c in range(cuts)], axis=1)


def local(event_items, event_sessions, sketch_bits):
    slabs = lax.axis_size("stream")
    slab = event_items.shape[0]
    total_events = slab * slabs
    words, band_size = sketch_bits.shape
    owned = band_size // slabs
    rows, width, half = 128, 256, owned // 4
    me = lax.axis_index("stream")
    own_start = me * owned
    first_id = lax.axis_index("item") * band_size + own_start
    blocks = slab // LANES
    length = total_events // LANES

    stacked = jnp.stack([event_items, event_sessions]).reshape(2, blocks, LANES)
    dma = pltpu.SemaphoreType.DMA
    events, head = pl.pallas_call(
        functools.partial(gather_kernel, slabs, rows, blocks),
        out_shape=(
            jax.ShapeDtypeStruct((slabs, 2, blocks, LANES), jnp.int32),
            jax.ShapeDtypeStruct((8, LANES), jnp.float32),
        ),
        in_specs=[VMEM],
        out_specs=(VMEM, VMEM),
        scratch_shapes=[
            pltpu.VMEM((2, 2, 8, LANES), jnp.int32),
            pltpu.VMEM((blocks + 16, LANES), jnp.int32),
            pltpu.VMEM((blocks + 16, LANES), jnp.int32),
            pltpu.VMEM((rows + 8, LANES), jnp.float32),
            pltpu.VMEM((8, LANES), jnp.float32),
            pltpu.VMEM((slabs, 8, LANES), jnp.float32),
            pltpu.VMEM((slabs, 8, LANES), jnp.float32),
            dma((slabs // 2,)),
            dma((slabs // 2,)),
            dma((slabs // 2,)),
            dma((slabs // 2,)),
            dma((2,)),
            dma((2,)),
            dma((slabs,)),
            dma((slabs,)),
        ],
        compiler_params=pltpu.CompilerParams(collective_id=0, has_side_effects=True),
        name="gather_events",
    )(stacked)

    band_rows = max(8, 2 * half // LANES)
    counts, margins = pl.pallas_call(
        functools.partial(tile_kernel, rows, length, half),
        out_shape=(
            jax.ShapeDtypeStruct((2, 2 * rows, half), jnp.float32),
            jax.ShapeDtypeStruct((2, band_rows, LANES), jnp.float32),
        ),
        in_specs=[pl.BlockSpec(memory_space=pltpu.SMEM), VMEM],
        out_specs=(VMEM, VMEM),
        scratch_shapes=[
            pltpu.VMEM((length, LANES), jnp.int32),
            pltpu.VMEM((length + 32, LANES), jnp.int32),
            pltpu.VMEM((2, length, LANES), jnp.float32),
        ],
        name="tile_counts",
    )(first_id.astype(jnp.int32)[None], events)

    own_rows = pl.pallas_call(
        functools.partial(sketch_kernel, slabs, rows, half, width, 1.0 / math.sqrt(total_events)),
        out_shape=jax.ShapeDtypeStruct((rows // slabs, width), jnp.float32),
        in_specs=[VMEM] * 3 + [pl.BlockSpec(memory_space=pl.ANY)],
        out_specs=VMEM,
        scratch_shapes=[
            pltpu.VMEM((2, band_rows, LANES), jnp.float32),
            pltpu.VMEM((words, owned), jnp.int32),
            pltpu.VMEM((words, rows), jnp.int32),
            pltpu.VMEM((rows, width), jnp.float32),
            pltpu.VMEM((slabs, 8, LANES), jnp.float32),
            pltpu.VMEM((slabs, 8, LANES), jnp.float32),
            dma((2,)),
            dma((slabs,)),
            dma((slabs,)),
        ],
        compiler_params=pltpu.CompilerParams(collective_id=1, has_side_effects=True),
        name="sketch_tile",
    )(counts, margins, head, sketch_bits)
    if lax.axis_size("item") > 1:
        own_rows = lax.psum(own_rows, "item")
    return own_rows


def solution(mesh):
    placed = (P("stream"), P("stream"), P(None, "item"))
    return jax.shard_map(
        local, mesh=mesh, in_specs=placed, out_specs=P("stream", None), check_vma=False
    )
```

time: 351 us -> 67.5 us (0.19)
  waiting for transfers between devices: 280 us -> 0 us
  Pallas kernels: 47.7 us -> 64.6 us
  between operations: 13.1 us -> 0.02 us
  other arithmetic: 5.85 us -> 1.34 us
    unnamed x4 -> x0, waiting for transfers between devices: 127 us -> none
    psum x1 -> x0, waiting for transfers between devices: 95.9 us -> none  [local(): head = lax.psum(head, 'stream')]
    all_gather x1 -> x0, waiting for transfers between devices: 56.6 us -> none  [local(): lax.all_gather(jnp.stack([event_items, event_sessions])[None], 'stream',...]
    pallas_call x2, Pallas kernels: 23.8 us -> 44.3 us  [the longest x1 26.1 us: local(): pl.pallas_call(functools.partial(gather_kernel, slabs, rows, blocks), out...]
    pallas_call x1, Pallas kernels: 24 us -> 20.3 us  [local(): pl.pallas_call(functools.partial(tile_kernel, rows, length, half), out_sh...]
    or x1 -> x0, other arithmetic: 3.58 us -> none  [local(): code = events[:, 0] | events[:, 1] << ITEM_BITS]
  transfers between devices with their start and end apart: 3 -> 0, of which waited for: 3 -> 0; matrix products, arithmetic and copies ran while one was open for 1% -> 0% of each run, Pallas kernels for 7% -> 0%
where the time goes in v2:
time: 67.5 us; the launch traced here: 67.2 us
  Pallas kernels  64.6 us (96%)
  other arithmetic  1.34 us (2%)
  local copies, waits for them, and re-layouts  1.27 us (2%)
    pallas_call x1, Pallas kernels, local(): pl.pallas_call(functools.partial(gather_kernel, slabs, rows, blocks), out...  26.1 us
    pallas_call x1, Pallas kernels, local(): pl.pallas_call(functools.partial(tile_kernel, rows, length, half), out_sh...  20.3 us
    pallas_call x1, Pallas kernels, local(): pl.pallas_call(functools.partial(sketch_kernel, slabs, rows, half, width,...  18.1 us

profile of v2, /device:TPU:0, one launch (start us, length us, event | category | flops | bytes accessed | tf_op | source)
XLA Modules:
  0.0 67.2 jit_solution(8678881716122152086)
XLA Ops:
  0.0 1.3 %pad_add_fusion.own_ref = s32[2,32,128]{2,1,0:T(8,128)} fusion(s32[1,32,128]{2,1,0:T(8,128)} %bitcast.3, s32[1,32,128]{2,1,0:T(8,128)} %bitcast.4), kind=kLoop, calls=%fused_computation | loop fusion | flops 8192 | bytes 65536 | tf_op jit(solution)/shard_map/stack | solution.py:372
  1.3 26.1 %gather_events.1 = (s32[32,2,32,128]{3,2,1,0:T(8,128)}, f32[8,128]{1,0:T(8,128)}) custom-call(s32[2,32,128]{2,1,0:T(8,128)} %pad_add_fusion.own_ref), custom_call_target="tpu_custom_call" | custom-call | tf_op jit(solution)/shard_map/gather_events/pallas_call | solution.py:374
  27.5 20.3 %tile_counts.1 = (f32[2,256,2048]{2,1,0:T(8,128)}, f32[2,32,128]{2,1,0:T(8,128)}) custom-call(s32[1]{0:T(128)} %bitcast.base_ref, s32[32,2,32,128]{3,2,1,0:T(8,128)} %get-tuple-element.9.all_ref), custom_call_target="tpu_custom_call" | custom-call | tf_op jit(solution)/shard_map/tile_counts/pallas_call | solution.py:404
  47.8 18.1 %sketch_tile.1 = f32[4,256]{1,0:T(4,128)} custom-call(f32[2,256,2048]{2,1,0:T(8,128)} %get-tuple-element.10.count_ref, f32[2,32,128]{2,1,0:T(8,128)} %get-tuple-element.11.margin_ref, f32[8,128]{1,0:T(8,128)} %get-tuple-element.12.head_ref, s32[15,262144]{1,0:T(8,128)} %bits_ref.1), custom_call_target="tpu_custom_call" | custom-call | tf_op jit(solution)/shard_map/sketch_tile/pallas_call | solution.py:420
  65.9 1.3 %copy.5 = f32[4,256]{1,0:T(4,128)} copy(f32[4,256]{1,0:T(4,128)} %sketch_tile.1) | data formatting | bytes 8192

commit v3 on v2

--- a/solution.py
+++ b/solution.py
@@ -13,12 +13,21 @@
 LANES = 128
 BITS_PER_WORD = 18
 BIG = 1.0e6
+VMEM_GRANT = 50 * 1024 * 1024
 NT = (((1,), (1,)), ((), ()))
 VMEM = pl.BlockSpec(memory_space=pltpu.VMEM)
 
 
 def one_where(mask):
     return jnp.where(mask, 1.0, 0.0).astype(jnp.bfloat16)
+
+
+def hot_columns(ids, values):
+    row = jnp.broadcast_to(values, (16, values.shape[1])).astype(jnp.bfloat16)
+    one, zero = jnp.ones((), jnp.bfloat16), jnp.zeros((), jnp.bfloat16)
+    return jnp.concatenate(
+        [jnp.where(ids[n : n + 16] == row, one, zero) for n in range(0, ids.shape[0], 16)], axis=0
+    )
 
 
 def greet_all(slabs, me):
@@ -214,13 +223,13 @@
     tally = lax.fori_loop(0, length // chunk, fill, (none, none))
     trips = (jnp.max(jnp.maximum(tally[0], tally[1])) + 1) // 2
 
-    row_ids = lax.broadcasted_iota(jnp.int32, (rows, 2 * LANES), 0).astype(jnp.float32)
+    row_ids = lax.broadcasted_iota(jnp.int32, (rows, 2 * LANES), 0).astype(jnp.float32).astype(jnp.bfloat16)
     d_ids = lax.broadcasted_iota(jnp.int32, (32, LANES), 0)
     near = (d_ids >= 1) & (d_ids != 16)
     m_ids = lax.broadcasted_iota(jnp.int32, (max(8, band_rows), 2 * LANES), 0)
     l_ids = lax.broadcasted_iota(jnp.int32, (LANES, 2 * LANES), 0)
-    tile = min(half, 512)
-    t_ids = lax.broadcasted_iota(jnp.int32, (tile, 2 * LANES), 0)
+    tile = 256
+    t_ids = lax.broadcasted_iota(jnp.int32, (tile, 2 * LANES), 0).astype(jnp.float32).astype(jnp.bfloat16)
 
     def body(unused, state):
         out = []
@@ -244,17 +253,18 @@
             head = jnp.concatenate(heads, axis=1)
             weight = jnp.concatenate(weights, axis=1)
             local = jnp.concatenate(locals_, axis=1)
-            links = jnp.zeros((rows, 2 * LANES), jnp.float32)
+            links = jnp.zeros((rows, 2 * LANES), jnp.bfloat16)
             for d in range(1, 32):
                 if d != 16:
-                    links += jnp.where(row_ids == head[d : d + 1], 1.0, 0.0)
+                    links += hot_columns(row_ids, head[d : d + 1])
             upper = local >= half
-            pair = jnp.concatenate(
-                [jnp.where(upper, 0.0, links), jnp.where(upper, links, 0.0)], axis=0
-            ).astype(jnp.bfloat16)
+            side = jnp.broadcast_to(jnp.where(upper, 1.0, 0.0), (16, 2 * LANES)).astype(jnp.bfloat16)
+            high_part = jnp.concatenate([links[n : n + 16] * side for n in range(0, rows, 16)], axis=0)
+            pair = jnp.concatenate([links - high_part, high_part], axis=0)
             inner = jnp.where(upper, local - half, local)
             for t in range(half // tile):
-                hot = one_where(t_ids + t * tile == inner)
+                inside = (inner >= t * tile) & (inner < (t + 1) * tile)
+                hot = hot_columns(t_ids, jnp.where(inside, inner - t * tile, -1).astype(jnp.float32))
                 count_ref[s, :, t * tile : (t + 1) * tile] += lax.dot_general(
                     pair, hot, NT, preferred_element_type=jnp.float32
                 )
@@ -396,7 +406,9 @@
             dma((slabs,)),
             dma((slabs,)),
         ],
-        compiler_params=pltpu.CompilerParams(collective_id=0, has_side_effects=True),
+        compiler_params=pltpu.CompilerParams(
+            collective_id=0, has_side_effects=True, vmem_limit_bytes=VMEM_GRANT
+        ),
         name="gather_events",
     )(stacked)
 
@@ -414,6 +426,7 @@
             pltpu.VMEM((length + 32, LANES), jnp.int32),
             pltpu.VMEM((2, length, LANES), jnp.float32),
         ],
+        compiler_params=pltpu.CompilerParams(vmem_limit_bytes=VMEM_GRANT),
         name="tile_counts",
     )(first_id.astype(jnp.int32)[None], events)
 
@@ -433,7 +446,9 @@
             dma((slabs,)),
             dma((slabs,)),
         ],
-        compiler_params=pltpu.CompilerParams(collective_id=1, has_side_effects=True),
+        compiler_params=pltpu.CompilerParams(
+            collective_id=1, has_side_effects=True, vmem_limit_bytes=VMEM_GRANT
+        ),
         name="sketch_tile",
     )(counts, margins, head, sketch_bits)
     if lax.axis_size("item") > 1:

time: 67.5 us -> 60.1 us (0.89); the launches traced: 67.2 us -> 59 us
  Pallas kernels: 64.6 us -> 57.7 us
    pallas_call x1, Pallas kernels: 20.3 us -> 15.8 us  [local(): pl.pallas_call(functools.partial(tile_kernel, rows, length, half), out_sh...]
    pallas_call x1, Pallas kernels: 26.1 us -> 24.5 us  [local(): pl.pallas_call(functools.partial(gather_kernel, slabs, rows, blocks), out...]
    pallas_call x1, Pallas kernels: 18.1 us -> 17.4 us  [local(): pl.pallas_call(functools.partial(sketch_kernel, slabs, rows, half, width,...]
where the time goes in v3:
time: 60.1 us; the launch traced here: 59 us
  Pallas kernels  57.7 us (96%)
  other arithmetic  0.74 us (1%)
    pallas_call x1, Pallas kernels, local(): pl.pallas_call(functools.partial(gather_kernel, slabs, rows, blocks), out...  24.5 us
    pallas_call x1, Pallas kernels, local(): pl.pallas_call(functools.partial(sketch_kernel, slabs, rows, half, width,...  17.4 us
    pallas_call x1, Pallas kernels, local(): pl.pallas_call(functools.partial(tile_kernel, rows, length, half), out_sh...  15.8 us

profile of v3, /device:TPU:0, one launch (start us, length us, event | category | flops | bytes accessed | tf_op | source)
XLA Modules:
  0.0 59.0 jit_solution(15724124632334533465)
XLA Ops:
  0.0 0.7 %pad_add_fusion.own_ref = s32[2,32,128]{2,1,0:T(8,128)S(1)} fusion(s32[1,32,128]{2,1,0:T(8,128)} %bitcast.3, s32[1,32,128]{2,1,0:T(8,128)} %bitcast.4), kind=kLoop, calls=%fused_computation | loop fusion | flops 8192 | bytes 65536 | tf_op jit(solution)/shard_map/stack | solution.py:382
  0.7 24.5 %gather_events.1 = (s32[32,2,32,128]{3,2,1,0:T(8,128)S(1)}, f32[8,128]{1,0:T(8,128)S(1)}) custom-call(s32[2,32,128]{2,1,0:T(8,128)S(1)} %pad_add_fusion.own_ref), custom_call_target="tpu_custom_call" | custom-call | tf_op jit(solution)/shard_map/gather_events/pallas_call | solution.py:384
  25.2 15.8 %tile_counts.1 = (f32[2,256,2048]{2,1,0:T(8,128)}, f32[2,32,128]{2,1,0:T(8,128)S(1)}) custom-call(s32[1]{0:T(128)} %bitcast.base_ref, s32[32,2,32,128]{3,2,1,0:T(8,128)S(1)} %get-tuple-element.9.all_ref), custom_call_target="tpu_custom_call" | custom-call | tf_op jit(solution)/shard_map/tile_counts/pallas_call | solution.py:416
  41.0 17.4 %sketch_tile.1 = f32[4,256]{1,0:T(4,128)S(1)} custom-call(f32[2,256,2048]{2,1,0:T(8,128)} %get-tuple-element.10.count_ref, f32[2,32,128]{2,1,0:T(8,128)S(1)} %get-tuple-element.11.margin_ref, f32[8,128]{1,0:T(8,128)S(1)} %get-tuple-element.12.head_ref, s32[15,262144]{1,0:T(8,128)} %bits_ref.1), custom_call_target="tpu_custom_call" | custom-call | tf_op jit(solution)/shard_map/sketch_tile/pallas_call | solution.py:433
  58.4 0.6 %copy.5 = f32[4,256]{1,0:T(4,128)} copy(f32[4,256]{1,0:T(4,128)S(1)} %sketch_tile.1) | data formatting | bytes 8192

commit v4 on v3

--- a/solution.py
+++ b/solution.py
@@ -13,7 +13,7 @@
 LANES = 128
 BITS_PER_WORD = 18
 BIG = 1.0e6
-VMEM_GRANT = 50 * 1024 * 1024
+VMEM_GRANT = 45 * 1024 * 1024
 NT = (((1,), (1,)), ((), ()))
 VMEM = pl.BlockSpec(memory_space=pltpu.VMEM)
 
@@ -75,40 +75,53 @@
 
 
 def gather_kernel(
-    slabs, rows, blocks, own_ref, all_ref, head_ref, halo_ref, item_ref, session_ref, links_ref, total_ref,
+    slabs, rows, blocks, own_items, own_sessions, all_items, all_sessions, head_ref,
+    short_ref, halo_ref, item_ref, session_ref, links_ref, total_ref,
     head_out, head_in, far_send, far_recv, near_send, near_recv, halo_send, halo_recv, head_send, head_recv,
 ):
     me = lax.axis_index("stream")
     partner = me + 1 - 2 * lax.rem(me, 2)
     after, before = lax.rem(me + 1, slabs), lax.rem(me + slabs - 1, slabs)
     barrier = greet_all(slabs, me)
+    short_ref[...] = own_sessions[...].astype(jnp.int16)
+    item_ref[8 : 8 + blocks] = own_items[...]
+    session_ref[8 : 8 + blocks] = own_sessions[...]
+    all_items[me] = own_items[...]
+    all_sessions[me] = short_ref[...]
     pl.semaphore_wait(barrier, slabs - 1)
 
-    low_halo = send(own_ref.at[:, blocks - 8 : blocks], halo_ref.at[0], halo_send.at[0], halo_recv.at[0], after)
-    high_halo = send(own_ref.at[:, 0:8], halo_ref.at[1], halo_send.at[1], halo_recv.at[1], before)
-    low_halo.start()
-    high_halo.start()
+    halos = []
+    for n, ref in enumerate((own_items, own_sessions)):
+        for side, to, rows_sent in ((0, after, ref.at[blocks - 8 : blocks]), (1, before, ref.at[0:8])):
+            at = 2 * n + side
+            halos.append(send(rows_sent, halo_ref.at[at], halo_send.at[at], halo_recv.at[at], to))
+    for copy in halos:
+        copy.start()
+
+    pairs = ((own_items, all_items, 0), (short_ref, all_sessions, slabs // 2))
 
     def far(k):
-        return send(own_ref, all_ref.at[me], far_send.at[k], far_recv.at[k], lax.rem(me + 2 * k, slabs))
+        to = lax.rem(me + 2 * k, slabs)
+        return [
+            send(own, every.at[me], far_send.at[at + k], far_recv.at[at + k], to) for own, every, at in pairs
+        ]
 
     def near(k):
         source = lax.rem(me + 2 * slabs - 2 * k, slabs)
-        return send(all_ref.at[source], all_ref.at[source], near_send.at[k], near_recv.at[k], partner)
-
-    own_near = send(own_ref, all_ref.at[me], near_send.at[0], near_recv.at[0], partner)
-    own_near.start()
-    each(1, slabs // 2, lambda k: far(k).start())
-    all_ref[me] = own_ref[...]
-
-    item_ref[8 : 8 + blocks] = own_ref[0]
-    session_ref[8 : 8 + blocks] = own_ref[1]
-    low_halo.wait()
-    high_halo.wait()
-    item_ref[0:8] = halo_ref[0, 0]
-    item_ref[8 + blocks : 16 + blocks] = halo_ref[1, 0]
-    session_ref[0:8] = jnp.where(me == 0, -1, halo_ref[0, 1])
-    session_ref[8 + blocks : 16 + blocks] = jnp.where(me == slabs - 1, -1, halo_ref[1, 1])
+        return [
+            send(every.at[source], every.at[source], near_send.at[at + k], near_recv.at[at + k], partner)
+            for own, every, at in pairs
+        ]
+
+    def do_all(copies, act):
+        for copy in copies:
+            act(copy)
+
+    own_near = [
+        send(own, every.at[me], near_send.at[at], near_recv.at[at], partner) for own, every, at in pairs
+    ]
+    each(1, slabs // 2, lambda k: do_all(far(k), lambda c: c.start()))
+    do_all(own_near, lambda c: c.start())
 
     sub = lax.broadcasted_iota(jnp.int32, (LANES, LANES), 0)
     lane = lax.broadcasted_iota(jnp.int32, (LANES, LANES), 1)
@@ -144,7 +157,15 @@
         total_ref[...] += links[rows:]
         return unused
 
-    lax.fori_loop(0, blocks, block, 0, unroll=4)
+    lax.fori_loop(1, blocks - 1, block, 0, unroll=5)
+    for copy in halos:
+        copy.wait()
+    item_ref[0:8] = halo_ref[0]
+    item_ref[8 + blocks : 16 + blocks] = halo_ref[1]
+    session_ref[0:8] = jnp.where(me == 0, -1, halo_ref[2])
+    session_ref[8 + blocks : 16 + blocks] = jnp.where(me == slabs - 1, -1, halo_ref[3])
+    block(0, 0)
+    block(blocks - 1, 0)
 
     share = rows // slabs
     tail = jnp.concatenate([links_ref[rows : rows + 1], total_ref[0:1]], axis=0)
@@ -156,15 +177,15 @@
     exchange(slabs, me, head_out, head_in, head_send, head_recv, True)
 
     def forward(k):
-        far(k).wait_recv()
-        near(k).start()
+        do_all(far(k), lambda c: c.wait_recv())
+        do_all(near(k), lambda c: c.start())
 
     each(1, slabs // 2, forward)
     exchange(slabs, me, head_out, head_in, head_send, head_recv, False)
     head_ref[...] = jnp.sum(head_in[...], axis=0)
-    own_near.wait()
-    each(1, slabs // 2, lambda k: near(k).wait())
-    each(1, slabs // 2, lambda k: far(k).wait_send())
+    do_all(own_near, lambda c: c.wait())
+    each(1, slabs // 2, lambda k: do_all(near(k), lambda c: c.wait()))
+    each(1, slabs // 2, lambda k: do_all(far(k), lambda c: c.wait_send()))
 
 
 def take_windows(code_ref, length, start):
@@ -187,7 +208,7 @@
     return value[0:32]
 
 
-def tile_kernel(rows, length, half, base_ref, all_ref, count_ref, margin_ref, flat_ref, code_ref, key_ref):
+def tile_kernel(rows, length, half, base_ref, all_items, all_sessions, count_ref, margin_ref, flat_ref, code_ref, key_ref):
     item_mask = (1 << ITEM_BITS) - 1
     base = base_ref[0]
     count_ref[...] = jnp.zeros_like(count_ref)
@@ -195,9 +216,9 @@
     band = 2 * half
     band_rows = band // LANES
     chunk = 8 * math.gcd(length // 8, 16)
-    blocks = all_ref.shape[2]
-    for n in range(all_ref.shape[0]):
-        flat_ref[n * blocks : (n + 1) * blocks] = all_ref[n, 0] | (all_ref[n, 1] << ITEM_BITS)
+    slabs, blocks, unused_lanes = all_items.shape
+    for n in range(slabs):
+        flat_ref[n * blocks : (n + 1) * blocks] = all_items[n] | (all_sessions[n].astype(jnp.int32) << ITEM_BITS)
     per = length // LANES
     for r in range(per):
         code_ref[16 + r * LANES : 16 + (r + 1) * LANES] = flat_ref[pl.ds(r, LANES, stride=per), :].T
@@ -379,30 +400,31 @@
     blocks = slab // LANES
     length = total_events // LANES
 
-    stacked = jnp.stack([event_items, event_sessions]).reshape(2, blocks, LANES)
     dma = pltpu.SemaphoreType.DMA
-    events, head = pl.pallas_call(
+    all_items, all_sessions, head = pl.pallas_call(
         functools.partial(gather_kernel, slabs, rows, blocks),
         out_shape=(
-            jax.ShapeDtypeStruct((slabs, 2, blocks, LANES), jnp.int32),
+            jax.ShapeDtypeStruct((slabs, blocks, LANES), jnp.int32),
+            jax.ShapeDtypeStruct((slabs, blocks, LANES), jnp.int16),
             jax.ShapeDtypeStruct((8, LANES), jnp.float32),
         ),
-        in_specs=[VMEM],
-        out_specs=(VMEM, VMEM),
+        in_specs=[VMEM, VMEM],
+        out_specs=(VMEM, VMEM, VMEM),
         scratch_shapes=[
-            pltpu.VMEM((2, 2, 8, LANES), jnp.int32),
+            pltpu.VMEM((blocks, LANES), jnp.int16),
+            pltpu.VMEM((4, 8, LANES), jnp.int32),
             pltpu.VMEM((blocks + 16, LANES), jnp.int32),
             pltpu.VMEM((blocks + 16, LANES), jnp.int32),
             pltpu.VMEM((rows + 8, LANES), jnp.float32),
             pltpu.VMEM((8, LANES), jnp.float32),
             pltpu.VMEM((slabs, 8, LANES), jnp.float32),
             pltpu.VMEM((slabs, 8, LANES), jnp.float32),
-            dma((slabs // 2,)),
-            dma((slabs // 2,)),
-            dma((slabs // 2,)),
-            dma((slabs // 2,)),
-            dma((2,)),
-            dma((2,)),
+            dma((slabs,)),
+            dma((slabs,)),
+            dma((slabs,)),
+            dma((slabs,)),
+            dma((4,)),
+            dma((4,)),
             dma((slabs,)),
             dma((slabs,)),
         ],
@@ -410,7 +432,7 @@
             collective_id=0, has_side_effects=True, vmem_limit_bytes=VMEM_GRANT
         ),
         name="gather_events",
-    )(stacked)
+    )(event_items.reshape(blocks, LANES), event_sessions.reshape(blocks, LANES))
 
     band_rows = max(8, 2 * half // LANES)
     counts, margins = pl.pallas_call(
@@ -419,7 +441,7 @@
             jax.ShapeDtypeStruct((2, 2 * rows, half), jnp.float32),
             jax.ShapeDtypeStruct((2, band_rows, LANES), jnp.float32),
         ),
-        in_specs=[pl.BlockSpec(memory_space=pltpu.SMEM), VMEM],
+        in_specs=[pl.BlockSpec(memory_space=pltpu.SMEM), VMEM, VMEM],
         out_specs=(VMEM, VMEM),
         scratch_shapes=[
             pltpu.VMEM((length, LANES), jnp.int32),
@@ -428,7 +450,7 @@
         ],
         compiler_params=pltpu.CompilerParams(vmem_limit_bytes=VMEM_GRANT),
         name="tile_counts",
-    )(first_id.astype(jnp.int32)[None], events)
+    )(first_id.astype(jnp.int32)[None], all_items, all_sessions)
 
     own_rows = pl.pallas_call(
         functools.partial(sketch_kernel, slabs, rows, half, width, 1.0 / math.sqrt(total_events)),

time: 60.1 us -> 55.9 us (0.930); the launches traced: 59 us -> 56.3 us
  Pallas kernels: 57.7 us -> 54.3 us
  local copies, waits for them, and re-layouts: 0.6 us -> 2.03 us
  other arithmetic: 0.74 us -> 0 us
    pallas_call x1, Pallas kernels: 24.5 us -> 21 us  [local(): pl.pallas_call(functools.partial(gather_kernel, slabs, rows, blocks), out...]
    unnamed x1 -> x5, local copies, waits for them, and re-layouts: 0.6 us -> 2.03 us
    another operation x1 -> x0, other arithmetic: 0.74 us -> none  [local(): stacked = jnp.stack([event_items, event_sessions]).reshape(2, blocks, LANES)]
where the time goes in v4:
time: 55.9 us; the launch traced here: 56.3 us
  Pallas kernels  54.3 us (97%)
  local copies, waits for them, and re-layouts  2.03 us (4%)
    pallas_call x1, Pallas kernels, local(): pl.pallas_call(functools.partial(gather_kernel, slabs, rows, blocks), out...  21 us
    pallas_call x1, Pallas kernels, local(): pl.pallas_call(functools.partial(sketch_kernel, slabs, rows, half, width,...  17.4 us
    pallas_call x1, Pallas kernels, local(): pl.pallas_call(functools.partial(tile_kernel, rows, length, half), out_sh...  15.8 us
    unnamed x5, local copies, waits for them, and re-layouts  2.03 us

profile of v4, /device:TPU:0, one launch (start us, length us, event | category | flops | bytes accessed | tf_op | source)
XLA Modules:
  0.0 56.3 jit_solution(2566653104987483621)
XLA Ops:
  0.0 0.0 copy-start
  0.0 0.7 %copy-done = s32[4096]{0:T(1024)S(1)} copy-done((s32[4096]{0:T(1024)S(1)}, s32[4096]{0:T(1024)}, u32[]{:S(2)}) %copy-start) | copy-done | bytes 16408
  0.7 0.0 copy-start.1
  0.7 0.7 %copy-done.1 = s32[4096]{0:T(1024)S(1)} copy-done((s32[4096]{0:T(1024)S(1)}, s32[4096]{0:T(1024)}, u32[]{:S(2)}) %copy-start.1) | copy-done | bytes 16408
  1.4 21.0 %gather_events.1 = (s32[32,32,128]{2,1,0:T(8,128)S(1)}, s16[32,32,128]{2,1,0:T(8,128)(2,1)S(1)}, f32[8,128]{1,0:T(8,128)S(1)}) custom-call(s32[32,128]{1,0:T(8,128)S(1)} %bitcast.3, s32[32,128]{1,0:T(8,128)S(1)} %bitcast.4), custom_call_target="tpu_custom_call" | custom-call | tf_op jit(solution)/shard_map/gather_events/pallas_call | solution.py:404
  22.5 15.8 %tile_counts.1 = (f32[2,256,2048]{2,1,0:T(8,128)S(1)}, f32[2,32,128]{2,1,0:T(8,128)S(1)}) custom-call(s32[1]{0:T(128)} %bitcast.base_ref, s32[32,32,128]{2,1,0:T(8,128)S(1)} %get-tuple-element.10.all_items, s16[32,32,128]{2,1,0:T(8,128)(2,1)S(1)} %get-tuple-element.11.all_sessions), custom_call_target="tpu_custom_call" | custom-call | tf_op jit(solution)/shard_map/tile_counts/pallas_call | solution.py:438
  38.3 17.4 %sketch_tile.1 = f32[4,256]{1,0:T(4,128)S(1)} custom-call(f32[2,256,2048]{2,1,0:T(8,128)S(1)} %get-tuple-element.12.count_ref, f32[2,32,128]{2,1,0:T(8,128)S(1)} %get-tuple-element.13.margin_ref, f32[8,128]{1,0:T(8,128)S(1)} %get-tuple-element.14.head_ref, s32[15,262144]{1,0:T(8,128)} %bits_ref.1), custom_call_target="tpu_custom_call" | custom-call | tf_op jit(solution)/shard_map/sketch_tile/pallas_call | solution.py:455
  55.7 0.6 %copy.5 = f32[4,256]{1,0:T(4,128)} copy(f32[4,256]{1,0:T(4,128)S(1)} %sketch_tile.1) | data formatting | bytes 8192
Async XLA Ops:
  0.0 0.7 %copy-start = (s32[4096]{0:T(1024)S(1)}, s32[4096]{0:T(1024)}, u32[]{:S(2)}) copy-start(s32[4096]{0:T(1024)} %param.3) | copy-start | bytes 49156
  0.7 0.7 %copy-start.1 = (s32[4096]{0:T(1024)S(1)}, s32[4096]{0:T(1024)}, u32[]{:S(2)}) copy-start(s32[4096]{0:T(1024)} %param.4) | copy-start | bytes 49156

commit v5 on v4

--- a/solution.py
+++ b/solution.py
@@ -33,13 +33,10 @@
 def greet_all(slabs, me):
     barrier = pltpu.get_barrier_semaphore()
 
-    def signal(k, unused):
+    for k in range(1, slabs):
         pl.semaphore_signal(
             barrier, inc=1, device_id={"stream": lax.rem(me + k, slabs)}, device_id_type=pl.DeviceIdType.MESH
         )
-        return unused
-
-    lax.fori_loop(1, slabs, signal, 0)
     return barrier
 
 
@@ -55,11 +52,8 @@
 
 
 def each(low, high, do):
-    def step(k, unused):
+    for k in range(low, high):
         do(k)
-        return unused
-
-    lax.fori_loop(low, high, step, 0)
 
 
 def exchange(slabs, me, out_ref, in_ref, send_sems, recv_sems, start):
@@ -75,13 +69,14 @@
 
 
 def gather_kernel(
-    slabs, rows, blocks, own_items, own_sessions, all_items, all_sessions, head_ref,
+    slabs, rows, blocks, own_ref, all_items, all_sessions, head_ref,
     short_ref, halo_ref, item_ref, session_ref, links_ref, total_ref,
     head_out, head_in, far_send, far_recv, near_send, near_recv, halo_send, halo_recv, head_send, head_recv,
 ):
     me = lax.axis_index("stream")
     partner = me + 1 - 2 * lax.rem(me, 2)
     after, before = lax.rem(me + 1, slabs), lax.rem(me + slabs - 1, slabs)
+    own_items, own_sessions = own_ref.at[0], own_ref.at[1]
     barrier = greet_all(slabs, me)
     short_ref[...] = own_sessions[...].astype(jnp.int16)
     item_ref[8 : 8 + blocks] = own_items[...]
@@ -327,18 +322,23 @@
 
     def product(positive, words):
         size = words.shape[1]
-        shift = lax.broadcasted_iota(jnp.int32, (8, size), 0)
+
+        def wide(value):
+            return jnp.concatenate([value] * (size // LANES), axis=1)
+
+        shift = lax.broadcasted_iota(jnp.int32, (8, LANES), 0)
         upper = positive.astype(jnp.bfloat16)
         lower = (positive - upper.astype(jnp.float32)).astype(jnp.bfloat16)
         parts = []
         for word, split, offset in groups:
             now = jnp.broadcast_to(words[word : word + 1], (8, size))
-            where_bit = shift + offset
+            where_bit = jnp.left_shift(1, shift + offset)
             if split < 8:
                 later = jnp.broadcast_to(words[word + 1 : word + 2], (8, size))
-                now = jnp.where(shift >= split, later, now)
-                where_bit = jnp.where(shift >= split, shift - split, where_bit)
-            parts.append(jnp.where(((now >> where_bit) & 1) == 1, 1.0, -1.0))
+                now = jnp.where(wide(shift) >= split, later, now)
+                place = jnp.where(shift >= split, shift - split, shift + offset)
+                where_bit = jnp.left_shift(1, place)
+            parts.append(jnp.where((now & wide(where_bit)) != 0, 1.0, -1.0))
         signs = jnp.concatenate(parts, axis=0).astype(jnp.bfloat16)
         both = jnp.concatenate([upper, lower], axis=0)
         value = lax.dot_general(both, signs, NT, preferred_element_type=jnp.float32)
@@ -408,7 +408,7 @@
             jax.ShapeDtypeStruct((slabs, blocks, LANES), jnp.int16),
             jax.ShapeDtypeStruct((8, LANES), jnp.float32),
         ),
-        in_specs=[VMEM, VMEM],
+        in_specs=[VMEM],
         out_specs=(VMEM, VMEM, VMEM),
         scratch_shapes=[
             pltpu.VMEM((blocks, LANES), jnp.int16),
@@ -432,7 +432,7 @@
             collective_id=0, has_side_effects=True, vmem_limit_bytes=VMEM_GRANT
         ),
         name="gather_events",
-    )(event_items.reshape(blocks, LANES), event_sessions.reshape(blocks, LANES))
+    )(jnp.stack([event_items, event_sessions]).reshape(2, blocks, LANES))
 
     band_rows = max(8, 2 * half // LANES)
     counts, margins = pl.pallas_call(

time: 55.9 us -> 53.2 us (0.952)
  Pallas kernels: 54.3 us -> 52.3 us
  local copies, waits for them, and re-layouts: 2.03 us -> 0.6 us
  other arithmetic: 0 us -> 0.74 us
    pallas_call x1, Pallas kernels: 17.4 us -> 15.5 us  [local(): pl.pallas_call(functools.partial(sketch_kernel, slabs, rows, half, width,...]
    unnamed x5 -> x1, local copies, waits for them, and re-layouts: 2.03 us -> 0.6 us
    another operation x0 -> x1, other arithmetic: none -> 0.74 us  [local(): jnp.stack([event_items, event_sessions]).reshape(2, blocks, LANES)]
where the time goes in v5:
time: 53.2 us; the launch traced here: 53.6 us
  Pallas kernels  52.3 us (98%)
  other arithmetic  0.74 us (1%)
  local copies, waits for them, and re-layouts  0.6 us (1%)
    pallas_call x1, Pallas kernels, local(): pl.pallas_call(functools.partial(gather_kernel, slabs, rows, blocks), out...  20.9 us
    pallas_call x1, Pallas kernels, local(): pl.pallas_call(functools.partial(tile_kernel, rows, length, half), out_sh...  15.8 us
    pallas_call x1, Pallas kernels, local(): pl.pallas_call(functools.partial(sketch_kernel, slabs, rows, half, width,...  15.5 us

profile of v5, /device:TPU:0, one launch (start us, length us, event | category | flops | bytes accessed | tf_op | source)
XLA Modules:
  0.0 53.6 jit_solution(11081584046622588783)
XLA Ops:
  0.0 0.7 %pad_add_fusion.own_ref = s32[2,32,128]{2,1,0:T(8,128)S(1)} fusion(s32[1,32,128]{2,1,0:T(8,128)} %bitcast.3, s32[1,32,128]{2,1,0:T(8,128)} %bitcast.4), kind=kLoop, calls=%fused_computation | loop fusion | flops 8192 | bytes 65536 | tf_op jit(solution)/shard_map/stack | solution.py:435
  0.7 20.9 %gather_events.1 = (s32[32,32,128]{2,1,0:T(8,128)S(1)}, s16[32,32,128]{2,1,0:T(8,128)(2,1)S(1)}, f32[8,128]{1,0:T(8,128)S(1)}) custom-call(s32[2,32,128]{2,1,0:T(8,128)S(1)} %pad_add_fusion.own_ref), custom_call_target="tpu_custom_call" | custom-call | tf_op jit(solution)/shard_map/gather_events/pallas_call | solution.py:404
  21.7 15.8 %tile_counts.1 = (f32[2,256,2048]{2,1,0:T(8,128)S(1)}, f32[2,32,128]{2,1,0:T(8,128)S(1)}) custom-call(s32[1]{0:T(128)} %bitcast.base_ref, s32[32,32,128]{2,1,0:T(8,128)S(1)} %get-tuple-element.10.all_items, s16[32,32,128]{2,1,0:T(8,128)(2,1)S(1)} %get-tuple-element.11.all_sessions), custom_call_target="tpu_custom_call" | custom-call | tf_op jit(solution)/shard_map/tile_counts/pallas_call | solution.py:438
  37.5 15.5 %sketch_tile.1 = f32[4,256]{1,0:T(4,128)S(1)} custom-call(f32[2,256,2048]{2,1,0:T(8,128)S(1)} %get-tuple-element.12.count_ref, f32[2,32,128]{2,1,0:T(8,128)S(1)} %get-tuple-element.13.margin_ref, f32[8,128]{1,0:T(8,128)S(1)} %get-tuple-element.14.head_ref, s32[15,262144]{1,0:T(8,128)} %bits_ref.1), custom_call_target="tpu_custom_call" | custom-call | tf_op jit(solution)/shard_map/sketch_tile/pallas_call | solution.py:455
  53.0 0.6 %copy.5 = f32[4,256]{1,0:T(4,128)} copy(f32[4,256]{1,0:T(4,128)S(1)} %sketch_tile.1) | data formatting | bytes 8192

commit v6 on v5

--- a/solution.py
+++ b/solution.py
@@ -372,7 +372,7 @@
                 acc_ref[...] += product(positive, own_bits[:, pl.ds(bit_at, tile)])
                 return unused
 
-            lax.fori_loop(0, half // tile, step, 0)
+            lax.fori_loop(0, half // tile, step, 0, unroll=True)
 
     cuts = width // LANES
     for d in range(slabs):

time: 53.2 us -> 51 us (0.959); the launches traced: 53.6 us -> 50.5 us
  Pallas kernels: 52.3 us -> 49.1 us
    pallas_call x1, Pallas kernels: 15.5 us -> 12.4 us  [local(): pl.pallas_call(functools.partial(sketch_kernel, slabs, rows, half, width,...]
where the time goes in v6:
time: 51 us; the launch traced here: 50.5 us
  Pallas kernels  49.1 us (96%)
  other arithmetic  0.74 us (1%)
  local copies, waits for them, and re-layouts  0.6 us (1%)
    pallas_call x1, Pallas kernels, local(): pl.pallas_call(functools.partial(gather_kernel, slabs, rows, blocks), out...  20.9 us
    pallas_call x1, Pallas kernels, local(): pl.pallas_call(functools.partial(tile_kernel, rows, length, half), out_sh...  15.8 us
    pallas_call x1, Pallas kernels, local(): pl.pallas_call(functools.partial(sketch_kernel, slabs, rows, half, width,...  12.4 us

profile of v6, /device:TPU:0, one launch (start us, length us, event | category | flops | bytes accessed | tf_op | source)
XLA Modules:
  0.0 50.5 jit_solution(5317546242454766697)
XLA Ops:
  0.0 0.7 %pad_add_fusion.own_ref = s32[2,32,128]{2,1,0:T(8,128)S(1)} fusion(s32[1,32,128]{2,1,0:T(8,128)} %bitcast.3, s32[1,32,128]{2,1,0:T(8,128)} %bitcast.4), kind=kLoop, calls=%fused_computation | loop fusion | flops 8192 | bytes 65536 | tf_op jit(solution)/shard_map/stack | solution.py:435
  0.7 20.9 %gather_events.1 = (s32[32,32,128]{2,1,0:T(8,128)S(1)}, s16[32,32,128]{2,1,0:T(8,128)(2,1)S(1)}, f32[8,128]{1,0:T(8,128)S(1)}) custom-call(s32[2,32,128]{2,1,0:T(8,128)S(1)} %pad_add_fusion.own_ref), custom_call_target="tpu_custom_call" | custom-call | tf_op jit(solution)/shard_map/gather_events/pallas_call | solution.py:404
  21.7 15.8 %tile_counts.1 = (f32[2,256,2048]{2,1,0:T(8,128)S(1)}, f32[2,32,128]{2,1,0:T(8,128)S(1)}) custom-call(s32[1]{0:T(128)} %bitcast.base_ref, s32[32,32,128]{2,1,0:T(8,128)S(1)} %get-tuple-element.10.all_items, s16[32,32,128]{2,1,0:T(8,128)(2,1)S(1)} %get-tuple-element.11.all_sessions), custom_call_target="tpu_custom_call" | custom-call | tf_op jit(solution)/shard_map/tile_counts/pallas_call | solution.py:438
  37.5 12.4 %sketch_tile.1 = f32[4,256]{1,0:T(4,128)S(1)} custom-call(f32[2,256,2048]{2,1,0:T(8,128)S(1)} %get-tuple-element.12.count_ref, f32[2,32,128]{2,1,0:T(8,128)S(1)} %get-tuple-element.13.margin_ref, f32[8,128]{1,0:T(8,128)S(1)} %get-tuple-element.14.head_ref, s32[15,262144]{1,0:T(8,128)} %bits_ref.1), custom_call_target="tpu_custom_call" | custom-call | tf_op jit(solution)/shard_map/sketch_tile/pallas_call | solution.py:455
  49.9 0.6 %copy.5 = f32[4,256]{1,0:T(4,128)} copy(f32[4,256]{1,0:T(4,128)S(1)} %sketch_tile.1) | data formatting | bytes 8192
